TPU v7x, 32 devices: a 4x4x1 block of a 4x4x8 slice. The times are simulated.
32 devices in a mesh: data: 1 (over z), stage: 32 (over y, x, core).
Axes of the slice: x: 4, y: 4, z: 1, core: 2. Of those that a mesh axis runs over, the one named last changes fastest.
The devices are a block of a 4x4x8 slice.
Arguments:
- micro_in: bfloat16 [32, 128, 512], P('data')
- targets: bfloat16 [32, 128, 512], P('data')
- w_in: bfloat16 [32, 2, 512, 1024], P('stage')
- w_out: bfloat16 [32, 2, 1024, 512], P('stage')
Outputs:
- output 1: float32 [32, 2, 512, 1024], P(('data', 'stage'))
- output 2: float32 [32, 2, 1024, 512], P(('data', 'stage'))
- output 3: float32 [1], P('data')
All inputs are finite; a program needn't handle non-finite values.
Results may differ from a plain program's by a relative error of at most 0.00710874.
Values are sent between devices in bfloat16 or wider.
A program may use at most 768 MiB of HBM per device.

v0:
```python
import functools
import jax
import jax.numpy as jnp
from jax import lax
from jax.sharding import PartitionSpec as P


def gelu_pair(pre_f32):
    gelu_val, pull_fn = jax.vjp(jax.nn.gelu, pre_f32)
    return gelu_val, pull_fn(jnp.ones_like(pre_f32))[0]


def layer_fwd(h_cur, w_a, w_b):
    pre_act = jnp.dot(h_cur, w_a, preferred_element_type=jnp.float32).astype(jnp.bfloat16)
    act_val = jax.nn.gelu(pre_act.astype(jnp.float32)).astype(jnp.bfloat16)
    branch = jnp.dot(act_val, w_b, preferred_element_type=jnp.float32)
    return (h_cur.astype(jnp.float32) + branch).astype(jnp.bfloat16), pre_act


def layer_bwd(grad_h, h_cur, pre_act, w_a, w_b):
    act_f32, gelu_slope = gelu_pair(pre_act.astype(jnp.float32))
    act_val = act_f32.astype(jnp.bfloat16)
    grad_act = jnp.einsum('bd,fd->bf', grad_h, w_b, preferred_element_type=jnp.float32)
    grad_pre = (gelu_slope * grad_act).astype(jnp.bfloat16)
    back_sum = jnp.einsum('bf,df->bd', grad_pre, w_a, preferred_element_type=jnp.float32)
    grad_in = (grad_h.astype(jnp.float32) + back_sum).astype(jnp.bfloat16)
    grad_wa = jnp.einsum('bd,bf->df', h_cur, grad_pre, preferred_element_type=jnp.float32)
    grad_wb = jnp.einsum('bf,bd->fd', act_val, grad_h, preferred_element_type=jnp.float32)
    return grad_in, grad_wa, grad_wb


def schedule(stage_id, slot_idx, stages, num_micro):
    warm_count = stages - stage_id
    lead_steps = slot_idx - stage_id
    half_lead = lead_steps // 2
    warm_ok = (lead_steps >= 0) & (lead_steps < jnp.minimum(warm_count, num_micro))
    steady_ok = (lead_steps >= 0) & (lead_steps % 2 == 0) & (half_lead >= warm_count) & (half_lead < num_micro)
    fwd_micro = jnp.where(warm_ok, lead_steps, half_lead)
    back_steps = slot_idx - (2 * stages - 1 - stage_id)
    bwd_micro = back_steps // 2
    bwd_ok = (back_steps >= 0) & (back_steps % 2 == 0) & (bwd_micro < num_micro)
    top_micro = num_micro - 1
    return warm_ok | steady_ok, jnp.clip(fwd_micro, 0, top_micro), bwd_ok, jnp.clip(bwd_micro, 0, top_micro)


def keep_state(run_state):
    return run_state


def solution(mesh):
    stages = mesh.shape['stage']
    down_pairs = [(src_idx, src_idx + 1) for src_idx in range(stages - 1)]
    up_pairs = [(src_idx + 1, src_idx) for src_idx in range(stages - 1)]

    def per_device(micro_in, targets, w_in, w_out):
        num_micro, tokens, model_dim = micro_in.shape
        hidden_dim = w_in.shape[-1]
        stage_idx = lax.axis_index('stage')
        is_first = stage_idx == 0
        is_last = stage_idx == stages - 1
        w_first = w_in[0]
        w_second = w_out[0]
        loss_scale = 1.0 / (num_micro * tokens * model_dim)

        def run_fwd(run_state, micro_idx):
            act_hold, grad_hold, saved_h, saved_pre, acc_a, acc_b, loss_acc, send_down, send_up = run_state
            x_now = lax.dynamic_index_in_dim(micro_in, micro_idx, 0, keepdims=False)
            h_first = jnp.where(is_first, x_now, act_hold)
            h_mid, pre_first = layer_fwd(h_first, w_first[0], w_second[0])
            h_out, pre_second = layer_fwd(h_mid, w_first[1], w_second[1])
            ring_idx = micro_idx % stages
            saved_h = lax.dynamic_update_index_in_dim(saved_h, jnp.stack([h_first, h_mid]), ring_idx, 0)
            saved_pre = lax.dynamic_update_index_in_dim(saved_pre, jnp.stack([pre_first, pre_second]), ring_idx, 0)
            tgt_now = lax.dynamic_index_in_dim(targets, micro_idx, 0, keepdims=False)
            residual = h_out.astype(jnp.float32) - tgt_now.astype(jnp.float32)
            loss_acc = loss_acc + jnp.where(is_last, 0.5 * jnp.sum(residual * residual) * loss_scale, 0.0)
            grad_hold = jnp.where(is_last, (residual * loss_scale).astype(jnp.bfloat16), grad_hold)
            return (act_hold, grad_hold, saved_h, saved_pre, acc_a, acc_b, loss_acc, h_out, send_up)

        def run_bwd(run_state, micro_idx):
            act_hold, grad_hold, saved_h, saved_pre, acc_a, acc_b, loss_acc, send_down, send_up = run_state
            ring_idx = micro_idx % stages
            h_pair = lax.dynamic_index_in_dim(saved_h, ring_idx, 0, keepdims=False)
            pre_pair = lax.dynamic_index_in_dim(saved_pre, ring_idx, 0, keepdims=False)
            grad_mid, grad_a_high, grad_b_high = layer_bwd(grad_hold, h_pair[1], pre_pair[1], w_first[1], w_second[1])
            grad_low, grad_a_low, grad_b_low = layer_bwd(grad_mid, h_pair[0], pre_pair[0], w_first[0], w_second[0])
            acc_a = acc_a + jnp.stack([grad_a_low, grad_a_high])
            acc_b = acc_b + jnp.stack([grad_b_low, grad_b_high])
            return (act_hold, grad_hold, saved_h, saved_pre, acc_a, acc_b, loss_acc, send_down, grad_low)

        def slot_body(slot_idx, run_state):
            fwd_ok, fwd_micro, bwd_ok, bwd_micro = schedule(stage_idx, slot_idx, stages, num_micro)
            run_state = lax.cond(fwd_ok, functools.partial(run_fwd, micro_idx=fwd_micro), keep_state, run_state)
            run_state = lax.cond(bwd_ok, functools.partial(run_bwd, micro_idx=bwd_micro), keep_state, run_state)
            act_hold, grad_hold, saved_h, saved_pre, acc_a, acc_b, loss_acc, send_down, send_up = run_state
            recv_act = lax.ppermute(send_down, 'stage', down_pairs)
            recv_grad = lax.ppermute(send_up, 'stage', up_pairs)
            prev_fwd = schedule(stage_idx - 1, slot_idx, stages, num_micro)[0]
            next_bwd = schedule(stage_idx + 1, slot_idx, stages, num_micro)[2]
            act_hold = jnp.where(prev_fwd & (stage_idx > 0), recv_act, act_hold)
            grad_hold = jnp.where(next_bwd & (stage_idx < stages - 1), recv_grad, grad_hold)
            return (act_hold, grad_hold, saved_h, saved_pre, acc_a, acc_b, loss_acc, send_down, send_up)

        block_zero = jnp.zeros((tokens, model_dim), jnp.bfloat16)
        init_state = (block_zero, block_zero, jnp.zeros((stages, 2, tokens, model_dim), jnp.bfloat16), jnp.zeros((stages, 2, tokens, hidden_dim), jnp.bfloat16), jnp.zeros((2, model_dim, hidden_dim), jnp.float32), jnp.zeros((2, hidden_dim, model_dim), jnp.float32), jnp.zeros((), jnp.float32), block_zero, block_zero)
        slot_count = 2 * num_micro + 2 * stages - 2
        final_state = lax.fori_loop(0, slot_count, slot_body, init_state)
        loss_total = lax.psum(final_state[6], 'stage')
        return final_state[4][None], final_state[5][None], loss_total.reshape(1)

    return jax.shard_map(per_device, mesh=mesh, in_specs=(P('data'), P('data'), P('stage'), P('stage')), out_specs=(P(('data', 'stage')), P(('data', 'stage')), P('data')), check_vma=False)
```

profile of v0, /device:TPU:96, one launch (start us, length us, event | category | flops | bytes accessed | tf_op | source)
XLA Modules:
  0.0 3389.8 jit_solution(13389317168156412919)
XLA Ops:
  16.7 3328.2 %while.33 = (s32[]{:T(128)}, bf16[128,512]{1,0:T(8,128)(2,1)S(1)}, bf16[128,512]{1,0:T(8,128)(2,1)S(1)}, bf16[32,2,128,512]{3,2,1,0:T(8,128)(2,1)}, bf16[32,2,12...) while((s32[]{:T(128)}, bf16[128,512]{1,0:T(8,128)(2,1)S(1)}, ...), condition=%wide.region_6.7_spmd.clone, body=%wide.region_0.6_spmd.clone.sunk | while | flops 1628962816 | bytes 103024712 | solution.py:107
  791.9 25.6 collective-permute-start
  826.3 54.8 %collective-permute-start = (bf16[128,512]{1,0:T(8,128)(2,1)}, bf16[128,512]{1,0:T(8,128)(2,1)S(1)}, u32[]{:S(2)}, u32[]{:S(2)}) collective-permute-start(bf16[128,512]{1,0:T(8,128)(2,1)} %get-tuple-element.1072), channel_id=1, source_target_pairs={{0,1},{1,2},{2,3},{3,4},{4,5},{5,6},{6,7},{7,8},{8,9},{9,10},{10,1... | collective-permute-start | bytes 393224 | tf_op jit(solution)/shard_map/while/body/eval_jaxpr/ppermute | solution.py:96
  891.8 55.2 %collective-permute-start = (bf16[128,512]{1,0:T(8,128)(2,1)}, bf16[128,512]{1,0:T(8,128)(2,1)S(1)}, u32[]{:S(2)}, u32[]{:S(2)}) collective-permute-start(bf16[128,512]{1,0:T(8,128)(2,1)} %get-tuple-element.1072), channel_id=1, source_target_pairs={{0,1},{1,2},{2,3},{3,4},{4,5},{5,6},{6,7},{7,8},{8,9},{9,10},{10,1... | collective-permute-start | bytes 393224 | tf_op jit(solution)/shard_map/while/body/eval_jaxpr/ppermute | solution.py:96
  959.4 51.2 %collective-permute-start = (bf16[128,512]{1,0:T(8,128)(2,1)}, bf16[128,512]{1,0:T(8,128)(2,1)S(1)}, u32[]{:S(2)}, u32[]{:S(2)}) collective-permute-start(bf16[128,512]{1,0:T(8,128)(2,1)} %get-tuple-element.1072), channel_id=1, source_target_pairs={{0,1},{1,2},{2,3},{3,4},{4,5},{5,6},{6,7},{7,8},{8,9},{9,10},{10,1... | collective-permute-start | bytes 393224 | tf_op jit(solution)/shard_map/while/body/eval_jaxpr/ppermute | solution.py:96
  1024.9 49.4 %collective-permute-start = (bf16[128,512]{1,0:T(8,128)(2,1)}, bf16[128,512]{1,0:T(8,128)(2,1)S(1)}, u32[]{:S(2)}, u32[]{:S(2)}) collective-permute-start(bf16[128,512]{1,0:T(8,128)(2,1)} %get-tuple-element.1072), channel_id=1, source_target_pairs={{0,1},{1,2},{2,3},{3,4},{4,5},{5,6},{6,7},{7,8},{8,9},{9,10},{10,1... | collective-permute-start | bytes 393224 | tf_op jit(solution)/shard_map/while/body/eval_jaxpr/ppermute | solution.py:96
  1090.4 47.7 %collective-permute-start = (bf16[128,512]{1,0:T(8,128)(2,1)}, bf16[128,512]{1,0:T(8,128)(2,1)S(1)}, u32[]{:S(2)}, u32[]{:S(2)}) collective-permute-start(bf16[128,512]{1,0:T(8,128)(2,1)} %get-tuple-element.1072), channel_id=1, source_target_pairs={{0,1},{1,2},{2,3},{3,4},{4,5},{5,6},{6,7},{7,8},{8,9},{9,10},{10,1... | collective-permute-start | bytes 393224 | tf_op jit(solution)/shard_map/while/body/eval_jaxpr/ppermute | solution.py:96
  1156.0 48.0 %collective-permute-start = (bf16[128,512]{1,0:T(8,128)(2,1)}, bf16[128,512]{1,0:T(8,128)(2,1)S(1)}, u32[]{:S(2)}, u32[]{:S(2)}) collective-permute-start(bf16[128,512]{1,0:T(8,128)(2,1)} %get-tuple-element.1072), channel_id=1, source_target_pairs={{0,1},{1,2},{2,3},{3,4},{4,5},{5,6},{6,7},{7,8},{8,9},{9,10},{10,1... | collective-permute-start | bytes 393224 | tf_op jit(solution)/shard_map/while/body/eval_jaxpr/ppermute | solution.py:96
  1223.7 44.0 %collective-permute-start = (bf16[128,512]{1,0:T(8,128)(2,1)}, bf16[128,512]{1,0:T(8,128)(2,1)S(1)}, u32[]{:S(2)}, u32[]{:S(2)}) collective-permute-start(bf16[128,512]{1,0:T(8,128)(2,1)} %get-tuple-element.1072), channel_id=1, source_target_pairs={{0,1},{1,2},{2,3},{3,4},{4,5},{5,6},{6,7},{7,8},{8,9},{9,10},{10,1... | collective-permute-start | bytes 393224 | tf_op jit(solution)/shard_map/while/body/eval_jaxpr/ppermute | solution.py:96
  1289.2 42.2 %collective-permute-start = (bf16[128,512]{1,0:T(8,128)(2,1)}, bf16[128,512]{1,0:T(8,128)(2,1)S(1)}, u32[]{:S(2)}, u32[]{:S(2)}) collective-permute-start(bf16[128,512]{1,0:T(8,128)(2,1)} %get-tuple-element.1072), channel_id=1, source_target_pairs={{0,1},{1,2},{2,3},{3,4},{4,5},{5,6},{6,7},{7,8},{8,9},{9,10},{10,1... | collective-permute-start | bytes 393224 | tf_op jit(solution)/shard_map/while/body/eval_jaxpr/ppermute | solution.py:96
  1332.9 21.6 collective-permute-done.1
  1354.7 40.4 %collective-permute-start = (bf16[128,512]{1,0:T(8,128)(2,1)}, bf16[128,512]{1,0:T(8,128)(2,1)S(1)}, u32[]{:S(2)}, u32[]{:S(2)}) collective-permute-start(bf16[128,512]{1,0:T(8,128)(2,1)} %get-tuple-element.1072), channel_id=1, source_target_pairs={{0,1},{1,2},{2,3},{3,4},{4,5},{5,6},{6,7},{7,8},{8,9},{9,10},{10,1... | collective-permute-start | bytes 393224 | tf_op jit(solution)/shard_map/while/body/eval_jaxpr/ppermute | solution.py:96
  1396.6 23.4 collective-permute-done.1
  1420.2 40.7 %collective-permute-start = (bf16[128,512]{1,0:T(8,128)(2,1)}, bf16[128,512]{1,0:T(8,128)(2,1)S(1)}, u32[]{:S(2)}, u32[]{:S(2)}) collective-permute-start(bf16[128,512]{1,0:T(8,128)(2,1)} %get-tuple-element.1072), channel_id=1, source_target_pairs={{0,1},{1,2},{2,3},{3,4},{4,5},{5,6},{6,7},{7,8},{8,9},{9,10},{10,1... | collective-permute-start | bytes 393224 | tf_op jit(solution)/shard_map/while/body/eval_jaxpr/ppermute | solution.py:96
  1462.5 25.2 collective-permute-done.1
  1487.9 36.8 %collective-permute-start = (bf16[128,512]{1,0:T(8,128)(2,1)}, bf16[128,512]{1,0:T(8,128)(2,1)S(1)}, u32[]{:S(2)}, u32[]{:S(2)}) collective-permute-start(bf16[128,512]{1,0:T(8,128)(2,1)} %get-tuple-element.1072), channel_id=1, source_target_pairs={{0,1},{1,2},{2,3},{3,4},{4,5},{5,6},{6,7},{7,8},{8,9},{9,10},{10,1... | collective-permute-start | bytes 393224 | tf_op jit(solution)/shard_map/while/body/eval_jaxpr/ppermute | solution.py:96
  1526.1 27.0 collective-permute-done.1
  1553.3 35.0 %collective-permute-start = (bf16[128,512]{1,0:T(8,128)(2,1)}, bf16[128,512]{1,0:T(8,128)(2,1)S(1)}, u32[]{:S(2)}, u32[]{:S(2)}) collective-permute-start(bf16[128,512]{1,0:T(8,128)(2,1)} %get-tuple-element.1072), channel_id=1, source_target_pairs={{0,1},{1,2},{2,3},{3,4},{4,5},{5,6},{6,7},{7,8},{8,9},{9,10},{10,1... | collective-permute-start | bytes 393224 | tf_op jit(solution)/shard_map/while/body/eval_jaxpr/ppermute | solution.py:96
  1589.8 28.9 collective-permute-done.1
  1659.2 23.0 collective-permute-done.1
  1716.7 20.0 collective-permute-done.1
  1771.1 20.0 collective-permute-done.1
  1825.6 20.0 collective-permute-done.1
  3344.9 44.9 %psum.7 = f32[1]{0:T(128)} all-reduce(f32[1]{0:T(128)} %bitcast.30), channel_id=1, replica_groups=mesh['data'=1,'stage'=32] {'stage'}, use_global_device_ids=true, to_apply=%region_7.8 | all-reduce | flops 1 | bytes 8 | tf_op jit(solution)/shard_map/psum | solution.py:108
  (1954 shorter events, 3395.0 us)
Async XLA Ops:
  791.9 27.1 collective-permute-start
  826.3 56.3 %collective-permute-start = (bf16[128,512]{1,0:T(8,128)(2,1)}, bf16[128,512]{1,0:T(8,128)(2,1)S(1)}, u32[]{:S(2)}, u32[]{:S(2)}) collective-permute-start(bf16[128,512]{1,0:T(8,128)(2,1)} %get-tuple-element.1072), channel_id=1, source_target_pairs={{0,1},{1,2},{2,3},{3,4},{4,5},{5,6},{6,7},{7,8},{8,9},{9,10},{10,1... | collective-permute-start | bytes 393224 | tf_op jit(solution)/shard_map/while/body/eval_jaxpr/ppermute | solution.py:96
  891.8 56.7 %collective-permute-start = (bf16[128,512]{1,0:T(8,128)(2,1)}, bf16[128,512]{1,0:T(8,128)(2,1)S(1)}, u32[]{:S(2)}, u32[]{:S(2)}) collective-permute-start(bf16[128,512]{1,0:T(8,128)(2,1)} %get-tuple-element.1072), channel_id=1, source_target_pairs={{0,1},{1,2},{2,3},{3,4},{4,5},{5,6},{6,7},{7,8},{8,9},{9,10},{10,1... | collective-permute-start | bytes 393224 | tf_op jit(solution)/shard_map/while/body/eval_jaxpr/ppermute | solution.py:96
  959.4 52.7 %collective-permute-start = (bf16[128,512]{1,0:T(8,128)(2,1)}, bf16[128,512]{1,0:T(8,128)(2,1)S(1)}, u32[]{:S(2)}, u32[]{:S(2)}) collective-permute-start(bf16[128,512]{1,0:T(8,128)(2,1)} %get-tuple-element.1072), channel_id=1, source_target_pairs={{0,1},{1,2},{2,3},{3,4},{4,5},{5,6},{6,7},{7,8},{8,9},{9,10},{10,1... | collective-permute-start | bytes 393224 | tf_op jit(solution)/shard_map/while/body/eval_jaxpr/ppermute | solution.py:96
  1024.9 50.9 %collective-permute-start = (bf16[128,512]{1,0:T(8,128)(2,1)}, bf16[128,512]{1,0:T(8,128)(2,1)S(1)}, u32[]{:S(2)}, u32[]{:S(2)}) collective-permute-start(bf16[128,512]{1,0:T(8,128)(2,1)} %get-tuple-element.1072), channel_id=1, source_target_pairs={{0,1},{1,2},{2,3},{3,4},{4,5},{5,6},{6,7},{7,8},{8,9},{9,10},{10,1... | collective-permute-start | bytes 393224 | tf_op jit(solution)/shard_map/while/body/eval_jaxpr/ppermute | solution.py:96
  1090.4 49.2 %collective-permute-start = (bf16[128,512]{1,0:T(8,128)(2,1)}, bf16[128,512]{1,0:T(8,128)(2,1)S(1)}, u32[]{:S(2)}, u32[]{:S(2)}) collective-permute-start(bf16[128,512]{1,0:T(8,128)(2,1)} %get-tuple-element.1072), channel_id=1, source_target_pairs={{0,1},{1,2},{2,3},{3,4},{4,5},{5,6},{6,7},{7,8},{8,9},{9,10},{10,1... | collective-permute-start | bytes 393224 | tf_op jit(solution)/shard_map/while/body/eval_jaxpr/ppermute | solution.py:96
  1156.0 49.5 %collective-permute-start = (bf16[128,512]{1,0:T(8,128)(2,1)}, bf16[128,512]{1,0:T(8,128)(2,1)S(1)}, u32[]{:S(2)}, u32[]{:S(2)}) collective-permute-start(bf16[128,512]{1,0:T(8,128)(2,1)} %get-tuple-element.1072), channel_id=1, source_target_pairs={{0,1},{1,2},{2,3},{3,4},{4,5},{5,6},{6,7},{7,8},{8,9},{9,10},{10,1... | collective-permute-start | bytes 393224 | tf_op jit(solution)/shard_map/while/body/eval_jaxpr/ppermute | solution.py:96
  1223.7 45.5 %collective-permute-start = (bf16[128,512]{1,0:T(8,128)(2,1)}, bf16[128,512]{1,0:T(8,128)(2,1)S(1)}, u32[]{:S(2)}, u32[]{:S(2)}) collective-permute-start(bf16[128,512]{1,0:T(8,128)(2,1)} %get-tuple-element.1072), channel_id=1, source_target_pairs={{0,1},{1,2},{2,3},{3,4},{4,5},{5,6},{6,7},{7,8},{8,9},{9,10},{10,1... | collective-permute-start | bytes 393224 | tf_op jit(solution)/shard_map/while/body/eval_jaxpr/ppermute | solution.py:96
  1289.2 43.7 %collective-permute-start = (bf16[128,512]{1,0:T(8,128)(2,1)}, bf16[128,512]{1,0:T(8,128)(2,1)S(1)}, u32[]{:S(2)}, u32[]{:S(2)}) collective-permute-start(bf16[128,512]{1,0:T(8,128)(2,1)} %get-tuple-element.1072), channel_id=1, source_target_pairs={{0,1},{1,2},{2,3},{3,4},{4,5},{5,6},{6,7},{7,8},{8,9},{9,10},{10,1... | collective-permute-start | bytes 393224 | tf_op jit(solution)/shard_map/while/body/eval_jaxpr/ppermute | solution.py:96
  1354.7 41.9 %collective-permute-start = (bf16[128,512]{1,0:T(8,128)(2,1)}, bf16[128,512]{1,0:T(8,128)(2,1)S(1)}, u32[]{:S(2)}, u32[]{:S(2)}) collective-permute-start(bf16[128,512]{1,0:T(8,128)(2,1)} %get-tuple-element.1072), channel_id=1, source_target_pairs={{0,1},{1,2},{2,3},{3,4},{4,5},{5,6},{6,7},{7,8},{8,9},{9,10},{10,1... | collective-permute-start | bytes 393224 | tf_op jit(solution)/shard_map/while/body/eval_jaxpr/ppermute | solution.py:96
  1420.2 42.2 %collective-permute-start = (bf16[128,512]{1,0:T(8,128)(2,1)}, bf16[128,512]{1,0:T(8,128)(2,1)S(1)}, u32[]{:S(2)}, u32[]{:S(2)}) collective-permute-start(bf16[128,512]{1,0:T(8,128)(2,1)} %get-tuple-element.1072), channel_id=1, source_target_pairs={{0,1},{1,2},{2,3},{3,4},{4,5},{5,6},{6,7},{7,8},{8,9},{9,10},{10,1... | collective-permute-start | bytes 393224 | tf_op jit(solution)/shard_map/while/body/eval_jaxpr/ppermute | solution.py:96
  1461.0 26.7 collective-permute-start.1
  1487.9 38.3 %collective-permute-start = (bf16[128,512]{1,0:T(8,128)(2,1)}, bf16[128,512]{1,0:T(8,128)(2,1)S(1)}, u32[]{:S(2)}, u32[]{:S(2)}) collective-permute-start(bf16[128,512]{1,0:T(8,128)(2,1)} %get-tuple-element.1072), channel_id=1, source_target_pairs={{0,1},{1,2},{2,3},{3,4},{4,5},{5,6},{6,7},{7,8},{8,9},{9,10},{10,1... | collective-permute-start | bytes 393224 | tf_op jit(solution)/shard_map/while/body/eval_jaxpr/ppermute | solution.py:96
  1524.7 28.5 collective-permute-start.1
  1553.3 36.5 %collective-permute-start = (bf16[128,512]{1,0:T(8,128)(2,1)}, bf16[128,512]{1,0:T(8,128)(2,1)S(1)}, u32[]{:S(2)}, u32[]{:S(2)}) collective-permute-start(bf16[128,512]{1,0:T(8,128)(2,1)} %get-tuple-element.1072), channel_id=1, source_target_pairs={{0,1},{1,2},{2,3},{3,4},{4,5},{5,6},{6,7},{7,8},{8,9},{9,10},{10,1... | collective-permute-start | bytes 393224 | tf_op jit(solution)/shard_map/while/body/eval_jaxpr/ppermute | solution.py:96
  1588.4 30.3 collective-permute-start.1
  1618.9 34.7 %collective-permute-start = (bf16[128,512]{1,0:T(8,128)(2,1)}, bf16[128,512]{1,0:T(8,128)(2,1)S(1)}, u32[]{:S(2)}, u32[]{:S(2)}) collective-permute-start(bf16[128,512]{1,0:T(8,128)(2,1)} %get-tuple-element.1072), channel_id=1, source_target_pairs={{0,1},{1,2},{2,3},{3,4},{4,5},{5,6},{6,7},{7,8},{8,9},{9,10},{10,1... | collective-permute-start | bytes 393224 | tf_op jit(solution)/shard_map/while/body/eval_jaxpr/ppermute | solution.py:96
  1736.8 25.6 collective-permute-start
  1791.2 25.6 collective-permute-start
  1845.7 25.6 collective-permute-start
  1900.1 25.6 collective-permute-start
  2009.0 25.6 collective-permute-start
  2063.5 25.6 collective-permute-start
  2118.0 25.6 collective-permute-start
  (357 other events, 2662.9 us)
where the time goes:
time: 3400 us; the launch traced here: 3390 us
  starting transfers between devices  1390 us (41%)
  waiting for transfers between devices  1010 us (30%)
  matrix products  462 us (14%)
  other arithmetic  345 us (10%)
  local copies, waits for them, and re-layouts  80.8 us (2%)
  loops' own time  60.8 us (2%)
  blocking collectives  44.9 us (1%)
    ppermute x126, starting transfers between devices, slot_body(): recv_act = lax.ppermute(send_down, 'stage', down_pairs)  1220 us
    ppermute x126, waiting for transfers between devices, slot_body(): recv_grad = lax.ppermute(send_up, 'stage', up_pairs)  1010 us
    ppermute x126, starting transfers between devices, slot_body(): recv_grad = lax.ppermute(send_up, 'stage', up_pairs)  164 us
    add x32, other arithmetic, run_bwd(): acc_a = acc_a + jnp.stack([grad_a_low, grad_a_high])  164 us
    dot_general x64, matrix products, layer_fwd(): branch = jnp.dot(act_val, w_b, preferred_element_type=jnp.float32)  114 us
    dot_general x64, matrix products, layer_bwd(): jnp.einsum('bd,fd->bf', grad_h, w_b, preferred_element_type=jnp.float32)  113 us
    dot_general x64, matrix products, layer_bwd(): jnp.einsum('bf,bd->fd', act_val, grad_h, preferred_element_type=jnp.float32)  96.9 us
    dot_general x64, matrix products, layer_bwd(): jnp.einsum('bd,bf->df', h_cur, grad_pre, preferred_element_type=jnp.float32)  87 us
  transfers between devices with their start and end apart: 252, of which 126 were waited for; matrix products, arithmetic and copies ran while one was open for 16% of the time, Pallas kernels for 0%

commit v1 on v0

v1 whole, which is shorter than its diff:
```python
import functools
import jax
import jax.numpy as jnp
from jax import lax
from jax.experimental import pallas as pl
from jax.experimental.pallas import tpu as pltpu
from jax.sharding import PartitionSpec as P

BF16 = jnp.bfloat16
F32 = jnp.float32
C0 = 0.7978845608028654
C1 = 0.044715 * C0
GROUP = 4
TILE = 256
RING = 20
SENDS = 4
SLOPE = 5
NEAR = 8


def gelu(x):
    return x * (0.5 + 0.5 * jnp.tanh(x * (C0 + C1 * (x * x))))


def gelu_pair(x):
    sq = x * x
    t = jnp.tanh(x * (C0 + C1 * sq))
    cdf = 0.5 + 0.5 * t
    slope = cdf + (x * (0.5 * C0 + 1.5 * C1 * sq)) * (1.0 - t * t)
    return x * cdf, slope


def tiles(width):
    return [slice(lo, lo + TILE) for lo in range(0, width, TILE)]


def kernel(stages, num_micro, ring, x_hbm, t_hbm, wa_hbm, wb_hbm, ga_out, gb_out, loss_out,
           wa, wb, wat, wbt, hh, uu, gg, ee, acc, act, et, hm, gm, gout, xt, lossv,
           f_recv, f_send, g_recv, g_send, w_sem, l_recv, l_send, o_sem):
    tokens, model = hh.shape[-2:]
    hidden = uu.shape[-1]
    me = lax.axis_index('stage')
    last = stages - 1
    is_last = me == last
    loss_scale = 1.0 / (num_micro * tokens * model)

    def weight_copies():
        return (pltpu.make_async_copy(wa_hbm, wa, w_sem.at[0]), pltpu.make_async_copy(wb_hbm, wb, w_sem.at[1]))

    for copy in weight_copies():
        copy.start()

    @pl.when(me == 0)
    def _():
        def load(j, c):
            pltpu.make_async_copy(x_hbm.at[j], hh.at[0, j], f_recv.at[j]).start()
            return c
        lax.fori_loop(0, num_micro, load, 0)

    @pl.when(is_last)
    def _():
        def load(j, c):
            pltpu.make_async_copy(t_hbm.at[j], gg.at[1, j], g_recv.at[j]).start()
            return c
        lax.fori_loop(0, num_micro, load, 0)
        lossv[...] = jnp.zeros_like(lossv)

    barrier = pltpu.get_barrier_semaphore()

    @pl.when(me > 0)
    def _():
        pl.semaphore_signal(barrier, inc=1, device_id={'stage': me - 1}, device_id_type=pl.DeviceIdType.MESH)

    @pl.when(me < last)
    def _():
        pl.semaphore_signal(barrier, inc=1, device_id={'stage': me + 1}, device_id_type=pl.DeviceIdType.MESH)

    pl.semaphore_wait(barrier, jnp.where((me == 0) | is_last, 1, 2))

    for copy in weight_copies():
        copy.wait()

    def send_fwd(j):
        return pltpu.make_async_remote_copy(
            src_ref=gg.at[0, j], dst_ref=hh.at[0, j], send_sem=f_send.at[j], recv_sem=f_recv.at[j],
            device_id={'stage': jnp.minimum(me + 1, last)}, device_id_type=pl.DeviceIdType.MESH)

    def send_bwd(i):
        slot = lax.rem(i, SENDS)
        return pltpu.make_async_remote_copy(
            src_ref=gout.at[slot], dst_ref=gg.at[1, i], send_sem=g_send.at[slot], recv_sem=g_recv.at[i],
            device_id={'stage': jnp.maximum(me - 1, 0)}, device_id_type=pl.DeviceIdType.MESH)

    def send_loss():
        return pltpu.make_async_remote_copy(
            src_ref=lossv, dst_ref=lossv, send_sem=l_send, recv_sem=l_recv,
            device_id={'stage': jnp.maximum(me - 1, 0)}, device_id_type=pl.DeviceIdType.MESH)

    def prepare():
        for l in range(2):
            for r in tiles(model):
                for c in tiles(hidden):
                    wat[l, c, r] = wa[l, r, c].T
                    wbt[l, r, c] = wb[l, c, r].T

        def clear(r, c):
            acc[r // (2 * model // 8), lax.rem(r // (model // 8), 2), pl.ds(lax.rem(r, model // 8) * 8, 8), :] = jnp.zeros((8, hidden), F32)
            return c
        lax.fori_loop(0, 4 * model // 8, clear, 0)

    def fwd_steps(j):
        def up(l, c):
            h = hh[0, j] if l == 0 else hm[...]
            pre = jnp.dot(h, wa[l, :, c], preferred_element_type=F32).astype(BF16)
            uu[l, j, :, c] = pre
            act[l, :, c] = gelu(pre.astype(F32)).astype(BF16)

        def down(l, c):
            h = hh[0, j, :, c] if l == 0 else hm[:, c]
            out = (h.astype(F32) + jnp.dot(act[l], wb[l, :, c], preferred_element_type=F32)).astype(BF16)
            if l == 0:
                hm[:, c] = out
                hh[1, j, :, c] = out
            else:
                gg[0, j, :, c] = out

        steps = []
        for l in range(2):
            steps.append([functools.partial(up, l, c) for c in tiles(hidden)])
            steps.append([functools.partial(down, l, c) for c in tiles(model)])
        return steps

    def bwd_steps(i):
        slot = lax.rem(i, ring)

        def up(l, c):
            g = gg[1, i] if l == 1 else gm[...]
            grad_act = jnp.dot(g, wbt[l, :, c], preferred_element_type=F32)
            val, slope = gelu_pair(uu[l, i, :, c].astype(F32))
            e = (slope * grad_act).astype(BF16)
            et[l, :, c] = e
            ee[l, slot, :, c] = e
            uu[l, i, :, c] = val.astype(BF16)

        def down(l, c):
            g = gg[1, i, :, c] if l == 1 else gm[:, c]
            out = (g.astype(F32) + jnp.dot(et[l], wat[l, :, c], preferred_element_type=F32)).astype(BF16)
            if l == 1:
                gm[:, c] = out
                gg[0, i, :, c] = out
            else:
                gout[lax.rem(i, SENDS), :, c] = out

        steps = []
        for l in (1, 0):
            steps.append([functools.partial(up, l, c) for c in tiles(hidden)])
            steps.append([functools.partial(down, l, c) for c in tiles(model)])
        return steps

    def wgt_steps(k):
        group = k // 4
        l = lax.rem(k // 2, 2)
        which = lax.rem(k, 2)
        return group, l, which

    def wgt(k, pick):
        group, l, _ = wgt_steps(k)
        first = group * GROUP
        rows = GROUP * tokens
        for r in tiles(rows):
            lo = first + r.start // tokens
            src = hh if pick == 0 else gg
            xt[:, r] = src[l, pl.ds(lo, TILE // tokens)].reshape(TILE, model).T
        out = []

        def piece(c):
            if pick == 0:
                y = ee[l, pl.ds(lax.rem(first, ring), GROUP), :, c]
            else:
                y = uu[l, pl.ds(first, GROUP), :, c]
            acc[pick, l, :, c] += jnp.dot(xt[...], y.reshape(rows, TILE), preferred_element_type=F32)

        return [functools.partial(piece, c) for c in tiles(hidden)]

    def run(*lists):
        for level in range(max(len(s) for s in lists)):
            parts = [s[level] for s in lists if level < len(s)]
            for at in range(max(len(p) for p in parts)):
                for p in parts:
                    if at < len(p):
                        p[at]()

    def wait_fwd(j):
        pltpu.make_async_copy(hh.at[0, j], hh.at[0, j], f_recv.at[j]).wait()

    def wait_bwd(i):
        @pl.when(is_last == False)
        def _():
            pltpu.make_async_copy(gg.at[1, i], gg.at[1, i], g_recv.at[i]).wait()
            send_fwd(i).wait_send()

        @pl.when((me > 0) & (i >= SENDS))
        def _():
            send_bwd(i - SENDS).wait_send()

    def ship_fwd(j):
        @pl.when(is_last == False)
        def _():
            send_fwd(j).start()

        @pl.when(is_last)
        def _():
            pltpu.make_async_copy(gg.at[1, j], gg.at[1, j], g_recv.at[j]).wait()
            res = gg[0, j].astype(F32) - gg[1, j].astype(F32)
            gg[1, j] = (res * loss_scale).astype(BF16)
            sq = jnp.sum((res * res).reshape(tokens // 8, 8, model), axis=0)
            part = sq[:, :128]
            for lo in range(128, model, 128):
                part = part + sq[:, lo:lo + 128]
            lossv[...] += part * (0.5 * loss_scale)

    def ship_bwd(i):
        @pl.when(me > 0)
        def _():
            send_bwd(i).start()

    warm = jnp.minimum(num_micro, 1 + SLOPE * (last - me))
    lag = jnp.where(me < NEAR, GROUP, ring - GROUP)
    prep_at = jnp.where(me == 0, num_micro, 0)

    def slot(t, carry):
        i = t - warm
        k = i - lag
        does_f = t < num_micro
        does_b = (i >= 0) & (i < num_micro)
        does_w = k >= 0
        which = lax.rem(k + 4, 2)

        @pl.when(t == prep_at)
        def _():
            prepare()

        @pl.when(i == num_micro - 1)
        def _():
            @pl.when(is_last == False)
            def _():
                pltpu.make_async_copy(lossv, lossv, l_recv).wait()

            @pl.when(me > 0)
            def _():
                send_loss().start()

        @pl.when(does_f)
        def _():
            wait_fwd(t)

        @pl.when(does_b)
        def _():
            wait_bwd(i)

        @pl.when(does_f & (i < 0))
        def _():
            run(fwd_steps(t))

        @pl.when(does_f & (i >= 0))
        def _():
            run(fwd_steps(t), bwd_steps(i))

        beside = does_b & (t >= num_micro)

        @pl.when(beside & (k < 0))
        def _():
            run(bwd_steps(i))

        for pick in range(2):
            @pl.when(beside & does_w & (which == pick))
            def _(pick=pick):
                pieces = wgt(k, pick)
                run(bwd_steps(i), [[p] for p in pieces])

        @pl.when(does_f)
        def _():
            ship_fwd(t)

        @pl.when(does_b)
        def _():
            ship_bwd(i)

        for pick in range(2):
            @pl.when(does_w & (beside == False) & (which == pick))
            def _(pick=pick):
                run([[p] for p in wgt(k, pick)])

        return carry

    lax.fori_loop(0, num_micro + warm + lag, slot, 0)

    outs = [pltpu.make_async_copy(acc.at[0], ga_out, o_sem.at[0]),
            pltpu.make_async_copy(acc.at[1], gb_out, o_sem.at[1]),
            pltpu.make_async_copy(lossv, loss_out, o_sem.at[2])]
    for copy in outs:
        copy.start()

    @pl.when(me > 0)
    def _():
        send_loss().wait_send()

        def drain(i, c):
            send_bwd(i).wait_send()
            return c
        lax.fori_loop(num_micro - SENDS, num_micro, drain, 0)

    for copy in outs:
        copy.wait()


def solution(mesh):
    stages = mesh.shape['stage']

    def per_device(micro_in, targets, w_in, w_out):
        num_micro, tokens, model = micro_in.shape
        hidden = w_in.shape[-1]
        ring = min(RING, num_micro)
        any_spec = pl.BlockSpec(memory_space=pl.ANY)
        dma = pltpu.SemaphoreType.DMA
        grad_a, grad_bt, loss = pl.pallas_call(
            functools.partial(kernel, stages, num_micro, ring),
            out_shape=(jax.ShapeDtypeStruct((2, model, hidden), F32), jax.ShapeDtypeStruct((2, model, hidden), F32), jax.ShapeDtypeStruct((8, 128), F32)),
            in_specs=[any_spec] * 4,
            out_specs=(any_spec,) * 3,
            scratch_shapes=[
                pltpu.VMEM((2, model, hidden), BF16),
                pltpu.VMEM((2, hidden, model), BF16),
                pltpu.VMEM((2, hidden, model), BF16),
                pltpu.VMEM((2, model, hidden), BF16),
                pltpu.VMEM((2, num_micro, tokens, model), BF16),
                pltpu.VMEM((2, num_micro, tokens, hidden), BF16),
                pltpu.VMEM((2, num_micro, tokens, model), BF16),
                pltpu.VMEM((2, ring, tokens, hidden), BF16),
                pltpu.VMEM((2, 2, model, hidden), F32),
                pltpu.VMEM((2, tokens, hidden), BF16),
                pltpu.VMEM((2, tokens, hidden), BF16),
                pltpu.VMEM((tokens, model), BF16),
                pltpu.VMEM((tokens, model), BF16),
                pltpu.VMEM((SENDS, tokens, model), BF16),
                pltpu.VMEM((model, GROUP * tokens), BF16),
                pltpu.VMEM((8, 128), F32),
                dma((num_micro,)), dma((num_micro,)), dma((num_micro,)), dma((SENDS,)),
                dma((2,)), dma(()), dma(()), dma((3,)),
            ],
            compiler_params=pltpu.CompilerParams(collective_id=0, has_side_effects=True, vmem_limit_bytes=67043328),
        )(micro_in, targets, w_in[0], w_out[0])
        return grad_a[None], jnp.swapaxes(grad_bt, 1, 2)[None], jnp.sum(loss).reshape(1)

    return jax.shard_map(per_device, mesh=mesh, in_specs=(P('data'), P('data'), P('stage'), P('stage')), out_specs=(P(('data', 'stage')), P(('data', 'stage')), P('data')), check_vma=False)
```

time: 3400 us -> 348 us (0.10)
  starting transfers between devices: 1390 us -> 0 us
  waiting for transfers between devices: 1010 us -> 0 us
  matrix products: 462 us -> 0 us
  other arithmetic: 345 us -> 1.28 us
  Pallas kernels: 0 us -> 335 us
  local copies, waits for them, and re-layouts: 80.8 us -> 10.2 us
  loops' own time: 60.8 us -> 0 us
  blocking collectives: 44.9 us -> 0 us
    ppermute x252 -> x0, starting transfers between devices: 1390 us -> none  [the longest x126 1220 us: slot_body(): recv_act = lax.ppermute(send_down, 'stage', down_pairs)]
    ppermute x252 -> x0, waiting for transfers between devices: 1010 us -> none  [the longest x126 1010 us: slot_body(): recv_grad = lax.ppermute(send_up, 'stage', up_pairs)]
    dot_general x384 -> x0, matrix products: 462 us -> none  [the longest x64 114 us: layer_fwd(): branch = jnp.dot(act_val, w_b, preferred_element_type=jnp.float32)]
    pallas_call x0 -> x1, Pallas kernels: none -> 335 us  [per_device(): pl.pallas_call(functools.partial(kernel, stages, num_micro, ring), out_sh...]
    add x64 -> x0, other arithmetic: 202 us -> none  [the longest x32 164 us: run_bwd(): acc_a = acc_a + jnp.stack([grad_a_low, grad_a_high])]
    cond x256 -> x0, local copies, waits for them, and re-layouts: 64.8 us -> none
    another operation x253 -> x0, loops' own time: 60.8 us -> none  [the longest x1 34.1 us: per_device(): final_state = lax.fori_loop(0, slot_count, slot_body, init_state)]
    dynamic_update_slice x64 -> x0, other arithmetic: 50.3 us -> none  [the longest x32 27 us: run_fwd(): lax.dynamic_update_index_in_dim(saved_pre, jnp.stack([pre_first, pre_seco...]
  transfers between devices with their start and end apart: 252 -> 0, of which waited for: 126 -> 0; matrix products, arithmetic and copies ran while one was open for 16% -> 0% of each run, Pallas kernels for 0% -> 0%
where the time goes in v1:
time: 348 us; the launch traced here: 347 us
  Pallas kernels  335 us (96%)
  local copies, waits for them, and re-layouts  10.2 us (3%)
    pallas_call x1, Pallas kernels, per_device(): pl.pallas_call(functools.partial(kernel, stages, num_micro, ring), out_sh...  335 us
    unnamed x2, local copies, waits for them, and re-layouts  10.2 us

profile of v1, /device:TPU:96, one launch (start us, length us, event | category | flops | bytes accessed | tf_op | source)
XLA Modules:
  0.0 347.3 jit_solution(16783952517886465172)
XLA Ops:
  0.6 335.3 %shard_map.67 = (f32[2,512,1024]{2,1,0:T(8,128)}, f32[2,512,1024]{2,1,0:T(8,128)}, f32[8,128]{1,0:T(8,128)}) custom-call(bf16[32,128,512]{2,1,0:T(8,128)(2,1)} %x_hbm.1, bf16[32,128,512]{2,1,0:T(8,128)(2,1)} %t_hbm.1, bf16[2,512,1024]{2,1,0:T(8,128)(2,1)} %bitcast.9, bf16[2,1024,512]{2,1,0:T(8,128)(2,1)} %bitcast.10), custom_call_target="tpu_custom_call" | custom-call | tf_op jit(solution)/shard_map/pallas_call | solution.py:326
  335.9 1.3 reduce_sum.9
  337.2 5.4 %copy.7 = f32[1,2,1024,512]{3,2,1,0:T(8,128)} copy(f32[1,2,1024,512]{2,3,1,0:T(8,128)} %bitcast.8) | data formatting | bytes 8388608
  342.5 4.8 %copy.9 = f32[1,2,512,1024]{3,2,1,0:T(8,128)} copy(f32[1,2,512,1024]{3,2,1,0:T(8,128)} %bitcast.7) | data formatting | bytes 8388608

commit v2 on v1

--- a/solution.py
+++ b/solution.py
@@ -12,10 +12,12 @@
 C1 = 0.044715 * C0
 GROUP = 4
 TILE = 256
-RING = 20
+RING = 24
 SENDS = 4
 SLOPE = 5
 NEAR = 8
+HALVES = 2
+MIX = 0
 
 
 def gelu(x):
@@ -44,6 +46,11 @@
     is_last = me == last
     loss_scale = 1.0 / (num_micro * tokens * model)
 
+    half = tokens // HALVES
+
+    def part(m):
+        return m // HALVES, pl.ds(pl.multiple_of(lax.rem(m, HALVES) * half, half), half)
+
     def weight_copies():
         return (pltpu.make_async_copy(wa_hbm, wa, w_sem.at[0]), pltpu.make_async_copy(wb_hbm, wb, w_sem.at[1]))
 
@@ -52,17 +59,19 @@
 
     @pl.when(me == 0)
     def _():
-        def load(j, c):
-            pltpu.make_async_copy(x_hbm.at[j], hh.at[0, j], f_recv.at[j]).start()
-            return c
-        lax.fori_loop(0, num_micro, load, 0)
+        def load(m, c):
+            j, rows = part(m)
+            pltpu.make_async_copy(x_hbm.at[j, rows], hh.at[0, j, rows], f_recv.at[m]).start()
+            return c
+        lax.fori_loop(0, num_micro * HALVES, load, 0)
 
     @pl.when(is_last)
     def _():
-        def load(j, c):
-            pltpu.make_async_copy(t_hbm.at[j], gg.at[1, j], g_recv.at[j]).start()
-            return c
-        lax.fori_loop(0, num_micro, load, 0)
+        def load(m, c):
+            j, rows = part(m)
+            pltpu.make_async_copy(t_hbm.at[j, rows], gg.at[1, j, rows], g_recv.at[m]).start()
+            return c
+        lax.fori_loop(0, num_micro * HALVES, load, 0)
         lossv[...] = jnp.zeros_like(lossv)
 
     barrier = pltpu.get_barrier_semaphore()
@@ -80,15 +89,17 @@
     for copy in weight_copies():
         copy.wait()
 
-    def send_fwd(j):
+    def send_fwd(m):
+        j, rows = part(m)
         return pltpu.make_async_remote_copy(
-            src_ref=gg.at[0, j], dst_ref=hh.at[0, j], send_sem=f_send.at[j], recv_sem=f_recv.at[j],
+            src_ref=gg.at[0, j, rows], dst_ref=hh.at[0, j, rows], send_sem=f_send.at[m], recv_sem=f_recv.at[m],
             device_id={'stage': jnp.minimum(me + 1, last)}, device_id_type=pl.DeviceIdType.MESH)
 
-    def send_bwd(i):
-        slot = lax.rem(i, SENDS)
+    def send_bwd(m):
+        i, rows = part(m)
         return pltpu.make_async_remote_copy(
-            src_ref=gout.at[slot], dst_ref=gg.at[1, i], send_sem=g_send.at[slot], recv_sem=g_recv.at[i],
+            src_ref=gout.at[lax.rem(i, SENDS), rows], dst_ref=gg.at[1, i, rows],
+            send_sem=g_send.at[lax.rem(m, SENDS * HALVES)], recv_sem=g_recv.at[m],
             device_id={'stage': jnp.maximum(me - 1, 0)}, device_id_type=pl.DeviceIdType.MESH)
 
     def send_loss():
@@ -108,21 +119,21 @@
             return c
         lax.fori_loop(0, 4 * model // 8, clear, 0)
 
-    def fwd_steps(j):
+    def fwd_steps(j, rows, n):
         def up(l, c):
-            h = hh[0, j] if l == 0 else hm[...]
+            h = hh[0, j, rows] if l == 0 else hm[:n]
             pre = jnp.dot(h, wa[l, :, c], preferred_element_type=F32).astype(BF16)
-            uu[l, j, :, c] = pre
-            act[l, :, c] = gelu(pre.astype(F32)).astype(BF16)
+            uu[l, j, rows, c] = pre
+            act[l, :n, c] = gelu(pre.astype(F32)).astype(BF16)
 
         def down(l, c):
-            h = hh[0, j, :, c] if l == 0 else hm[:, c]
-            out = (h.astype(F32) + jnp.dot(act[l], wb[l, :, c], preferred_element_type=F32)).astype(BF16)
+            h = hh[0, j, rows, c] if l == 0 else hm[:n, c]
+            out = (h.astype(F32) + jnp.dot(act[l, :n], wb[l, :, c], preferred_element_type=F32)).astype(BF16)
             if l == 0:
-                hm[:, c] = out
-                hh[1, j, :, c] = out
+                hm[:n, c] = out
+                hh[1, j, rows, c] = out
             else:
-                gg[0, j, :, c] = out
+                gg[0, j, rows, c] = out
 
         steps = []
         for l in range(2):
@@ -130,26 +141,26 @@
             steps.append([functools.partial(down, l, c) for c in tiles(model)])
         return steps
 
-    def bwd_steps(i):
+    def bwd_steps(i, rows, n):
         slot = lax.rem(i, ring)
 
         def up(l, c):
-            g = gg[1, i] if l == 1 else gm[...]
+            g = gg[1, i, rows] if l == 1 else gm[:n]
             grad_act = jnp.dot(g, wbt[l, :, c], preferred_element_type=F32)
-            val, slope = gelu_pair(uu[l, i, :, c].astype(F32))
+            val, slope = gelu_pair(uu[l, i, rows, c].astype(F32))
             e = (slope * grad_act).astype(BF16)
-            et[l, :, c] = e
-            ee[l, slot, :, c] = e
-            uu[l, i, :, c] = val.astype(BF16)
+            et[l, :n, c] = e
+            ee[l, slot, rows, c] = e
+            uu[l, i, rows, c] = val.astype(BF16)
 
         def down(l, c):
-            g = gg[1, i, :, c] if l == 1 else gm[:, c]
-            out = (g.astype(F32) + jnp.dot(et[l], wat[l, :, c], preferred_element_type=F32)).astype(BF16)
+            g = gg[1, i, rows, c] if l == 1 else gm[:n, c]
+            out = (g.astype(F32) + jnp.dot(et[l, :n], wat[l, :, c], preferred_element_type=F32)).astype(BF16)
             if l == 1:
-                gm[:, c] = out
-                gg[0, i, :, c] = out
+                gm[:n, c] = out
+                gg[0, i, rows, c] = out
             else:
-                gout[lax.rem(i, SENDS), :, c] = out
+                gout[lax.rem(i, SENDS), rows, c] = out
 
         steps = []
         for l in (1, 0):
@@ -157,15 +168,9 @@
             steps.append([functools.partial(down, l, c) for c in tiles(model)])
         return steps
 
-    def wgt_steps(k):
-        group = k // 4
+    def wgt(k, pick):
         l = lax.rem(k // 2, 2)
-        which = lax.rem(k, 2)
-        return group, l, which
-
-    def wgt(k, pick):
-        group, l, _ = wgt_steps(k)
-        first = group * GROUP
+        first = (k // 4) * GROUP
         rows = GROUP * tokens
         for r in tiles(rows):
             lo = first + r.start // tokens
@@ -183,46 +188,61 @@
         return [functools.partial(piece, c) for c in tiles(hidden)]
 
     def run(*lists):
+        if MIX == 0:
+            lists = [sum(lists, [])]
         for level in range(max(len(s) for s in lists)):
             parts = [s[level] for s in lists if level < len(s)]
+            if MIX < 2:
+                parts = [sum(parts, [])]
             for at in range(max(len(p) for p in parts)):
                 for p in parts:
                     if at < len(p):
                         p[at]()
 
-    def wait_fwd(j):
-        pltpu.make_async_copy(hh.at[0, j], hh.at[0, j], f_recv.at[j]).wait()
-
-    def wait_bwd(i):
+    def wait_fwd(m):
+        j, rows = part(m)
+        pltpu.make_async_copy(hh.at[0, j, rows], hh.at[0, j, rows], f_recv.at[m]).wait()
+
+    def wait_bwd(m):
+        i, rows = part(m)
+
         @pl.when(is_last == False)
         def _():
-            pltpu.make_async_copy(gg.at[1, i], gg.at[1, i], g_recv.at[i]).wait()
-            send_fwd(i).wait_send()
-
-        @pl.when((me > 0) & (i >= SENDS))
-        def _():
-            send_bwd(i - SENDS).wait_send()
-
-    def ship_fwd(j):
+            pltpu.make_async_copy(gg.at[1, i, rows], gg.at[1, i, rows], g_recv.at[m]).wait()
+            send_fwd(m).wait_send()
+
+        @pl.when((me > 0) & (m >= SENDS * HALVES))
+        def _():
+            send_bwd(m - SENDS * HALVES).wait_send()
+
+    def ship_fwd(m):
+        j, rows = part(m)
+
         @pl.when(is_last == False)
         def _():
-            send_fwd(j).start()
+            send_fwd(m).start()
 
         @pl.when(is_last)
         def _():
-            pltpu.make_async_copy(gg.at[1, j], gg.at[1, j], g_recv.at[j]).wait()
-            res = gg[0, j].astype(F32) - gg[1, j].astype(F32)
-            gg[1, j] = (res * loss_scale).astype(BF16)
-            sq = jnp.sum((res * res).reshape(tokens // 8, 8, model), axis=0)
-            part = sq[:, :128]
+            pltpu.make_async_copy(gg.at[1, j, rows], gg.at[1, j, rows], g_recv.at[m]).wait()
+            res = gg[0, j, rows].astype(F32) - gg[1, j, rows].astype(F32)
+            gg[1, j, rows] = (res * loss_scale).astype(BF16)
+            sq = jnp.sum((res * res).reshape(half // 8, 8, model), axis=0)
+            total = sq[:, :128]
             for lo in range(128, model, 128):
-                part = part + sq[:, lo:lo + 128]
-            lossv[...] += part * (0.5 * loss_scale)
-
-    def ship_bwd(i):
+                total = total + sq[:, lo:lo + 128]
+            lossv[...] += total * (0.5 * loss_scale)
+
+    def ship_bwd(m):
         @pl.when(me > 0)
         def _():
-            send_bwd(i).start()
+            send_bwd(m).start()
+
+    def each(j, body):
+        def step(b, c):
+            body(j * HALVES + b)
+            return c
+        lax.fori_loop(0, HALVES, step, 0)
 
     warm = jnp.minimum(num_micro, 1 + SLOPE * (last - me))
     lag = jnp.where(me < NEAR, GROUP, ring - GROUP)
@@ -250,46 +270,36 @@
             def _():
                 send_loss().start()
 
-        @pl.when(does_f)
-        def _():
-            wait_fwd(t)
-
-        @pl.when(does_b)
-        def _():
-            wait_bwd(i)
-
         @pl.when(does_f & (i < 0))
         def _():
-            run(fwd_steps(t))
+            def step(m):
+                wait_fwd(m)
+                run(fwd_steps(*part(m), half))
+                ship_fwd(m)
+            each(t, step)
 
         @pl.when(does_f & (i >= 0))
         def _():
-            run(fwd_steps(t), bwd_steps(i))
-
-        beside = does_b & (t >= num_micro)
-
-        @pl.when(beside & (k < 0))
-        def _():
-            run(bwd_steps(i))
+            rows = slice(None)
+            each(t, wait_fwd)
+            each(i, wait_bwd)
+            run(fwd_steps(t, rows, tokens), bwd_steps(i, rows, tokens))
+            each(i, ship_bwd)
+            each(t, ship_fwd)
+
+        @pl.when(does_b & (t >= num_micro))
+        def _():
+            def step(m):
+                wait_bwd(m)
+                run(bwd_steps(*part(m), half))
+                ship_bwd(m)
+            each(i, step)
 
         for pick in range(2):
-            @pl.when(beside & does_w & (which == pick))
+            @pl.when(does_w & (which == pick))
             def _(pick=pick):
-                pieces = wgt(k, pick)
-                run(bwd_steps(i), [[p] for p in pieces])
-
-        @pl.when(does_f)
-        def _():
-            ship_fwd(t)
-
-        @pl.when(does_b)
-        def _():
-            ship_bwd(i)
-
-        for pick in range(2):
-            @pl.when(does_w & (beside == False) & (which == pick))
-            def _(pick=pick):
-                run([[p] for p in wgt(k, pick)])
+                for piece in wgt(k, pick):
+                    piece()
 
         return carry
 
@@ -305,10 +315,10 @@
     def _():
         send_loss().wait_send()
 
-        def drain(i, c):
-            send_bwd(i).wait_send()
-            return c
-        lax.fori_loop(num_micro - SENDS, num_micro, drain, 0)
+        def drain(m, c):
+            send_bwd(m).wait_send()
+            return c
+        lax.fori_loop((num_micro - SENDS) * HALVES, num_micro * HALVES, drain, 0)
 
     for copy in outs:
         copy.wait()
@@ -345,7 +355,7 @@
                 pltpu.VMEM((SENDS, tokens, model), BF16),
                 pltpu.VMEM((model, GROUP * tokens), BF16),
                 pltpu.VMEM((8, 128), F32),
-                dma((num_micro,)), dma((num_micro,)), dma((num_micro,)), dma((SENDS,)),
+                dma((num_micro * HALVES,)), dma((num_micro * HALVES,)), dma((num_micro * HALVES,)), dma((SENDS * HALVES,)),
                 dma((2,)), dma(()), dma(()), dma((3,)),
             ],
             compiler_params=pltpu.CompilerParams(collective_id=0, has_side_effects=True, vmem_limit_bytes=67043328),

time: 348 us -> 328 us (0.943)
  Pallas kernels: 335 us -> 316 us
    pallas_call x1, Pallas kernels: 335 us -> 316 us  [per_device(): pl.pallas_call(functools.partial(kernel, stages, num_micro, ring), out_sh...]
where the time goes in v2:
time: 328 us
  Pallas kernels  316 us (96%)
  local copies, waits for them, and re-layouts  10.2 us (3%)
    pallas_call x1, Pallas kernels, per_device(): pl.pallas_call(functools.partial(kernel, stages, num_micro, ring), out_sh...  316 us
    unnamed x2, local copies, waits for them, and re-layouts  10.2 us

profile of v2, /device:TPU:96, one launch (start us, length us, event | category | flops | bytes accessed | tf_op | source)
XLA Modules:
  0.0 327.7 jit_solution(22079047840254868)
XLA Ops:
  0.6 315.6 %shard_map.67 = (f32[2,512,1024]{2,1,0:T(8,128)}, f32[2,512,1024]{2,1,0:T(8,128)}, f32[8,128]{1,0:T(8,128)}) custom-call(bf16[32,128,512]{2,1,0:T(8,128)(2,1)} %x_hbm.1, bf16[32,128,512]{2,1,0:T(8,128)(2,1)} %t_hbm.1, bf16[2,512,1024]{2,1,0:T(8,128)(2,1)} %bitcast.9, bf16[2,1024,512]{2,1,0:T(8,128)(2,1)} %bitcast.10), custom_call_target="tpu_custom_call" | custom-call | tf_op jit(solution)/shard_map/pallas_call | solution.py:336
  316.2 1.3 reduce_sum.9
  317.5 5.4 %copy.7 = f32[1,2,1024,512]{3,2,1,0:T(8,128)} copy(f32[1,2,1024,512]{2,3,1,0:T(8,128)} %bitcast.8) | data formatting | bytes 8388608
  322.9 4.8 %copy.9 = f32[1,2,512,1024]{3,2,1,0:T(8,128)} copy(f32[1,2,512,1024]{3,2,1,0:T(8,128)} %bitcast.7) | data formatting | bytes 8388608

commit v3 on v2

--- a/solution.py
+++ b/solution.py
@@ -12,12 +12,12 @@
 C1 = 0.044715 * C0
 GROUP = 4
 TILE = 256
-RING = 24
+RING = 8
 SENDS = 4
-SLOPE = 5
+PAIR_SLACK = 3
+CHIP_SLACK = 7
 NEAR = 8
 HALVES = 2
-MIX = 0
 
 
 def gelu(x):
@@ -36,9 +36,9 @@
     return [slice(lo, lo + TILE) for lo in range(0, width, TILE)]
 
 
-def kernel(stages, num_micro, ring, x_hbm, t_hbm, wa_hbm, wb_hbm, ga_out, gb_out, loss_out,
-           wa, wb, wat, wbt, hh, uu, gg, ee, acc, act, et, hm, gm, gout, xt, lossv,
-           f_recv, f_send, g_recv, g_send, w_sem, l_recv, l_send, o_sem):
+def kernel(stages, num_micro, ring, x_hbm, t_hbm, wa_hbm, wb_hbm, ga_out, gb_out, loss_out, e_hbm,
+           wa, wb, wat, wbt, hh, uu, gg, ee, es, acc, act, et, hm, gm, gout, xt, lossv,
+           f_recv, f_send, g_recv, g_send, w_sem, l_recv, l_send, o_sem, e_out, e_in):
     tokens, model = hh.shape[-2:]
     hidden = uu.shape[-1]
     me = lax.axis_index('stage')
@@ -168,7 +168,19 @@
             steps.append([functools.partial(down, l, c) for c in tiles(model)])
         return steps
 
-    def wgt(k, pick):
+    def store_e(i):
+        slot = lax.rem(i, ring)
+        return pltpu.make_async_copy(ee.at[:, slot], e_hbm.at[:, i], e_out.at[slot])
+
+    def load_e(k):
+        l, first, buf = lax.rem(k // 2, 2), (k // 4) * GROUP, lax.rem(k // 2, 2)
+        return pltpu.make_async_copy(e_hbm.at[l, pl.ds(first, GROUP)], es.at[buf], e_in.at[buf])
+
+    def result(k, pick):
+        l = lax.rem(k // 2, 2)
+        return pltpu.make_async_copy(acc.at[pick, l], (ga_out, gb_out)[pick].at[l], o_sem.at[pick, l])
+
+    def wgt(k, pick, direct):
         l = lax.rem(k // 2, 2)
         first = (k // 4) * GROUP
         rows = GROUP * tokens
@@ -176,28 +188,24 @@
             lo = first + r.start // tokens
             src = hh if pick == 0 else gg
             xt[:, r] = src[l, pl.ds(lo, TILE // tokens)].reshape(TILE, model).T
-        out = []
 
         def piece(c):
-            if pick == 0:
+            if pick == 0 and direct:
                 y = ee[l, pl.ds(lax.rem(first, ring), GROUP), :, c]
+            elif pick == 0:
+                y = es[lax.rem(k // 2, 2), :, :, c]
             else:
                 y = uu[l, pl.ds(first, GROUP), :, c]
             acc[pick, l, :, c] += jnp.dot(xt[...], y.reshape(rows, TILE), preferred_element_type=F32)
 
-        return [functools.partial(piece, c) for c in tiles(hidden)]
+        for c in tiles(hidden):
+            piece(c)
 
     def run(*lists):
-        if MIX == 0:
-            lists = [sum(lists, [])]
-        for level in range(max(len(s) for s in lists)):
-            parts = [s[level] for s in lists if level < len(s)]
-            if MIX < 2:
-                parts = [sum(parts, [])]
-            for at in range(max(len(p) for p in parts)):
-                for p in parts:
-                    if at < len(p):
-                        p[at]()
+        for steps in lists:
+            for pieces in steps:
+                for piece in pieces:
+                    piece()
 
     def wait_fwd(m):
         j, rows = part(m)
@@ -244,8 +252,9 @@
             return c
         lax.fori_loop(0, HALVES, step, 0)
 
-    warm = jnp.minimum(num_micro, 1 + SLOPE * (last - me))
-    lag = jnp.where(me < NEAR, GROUP, ring - GROUP)
+    warm = jnp.minimum(num_micro, 1 + PAIR_SLACK * ((last - me + 1) // 2) + CHIP_SLACK * ((last - me) // 2))
+    near = me < NEAR
+    lag = jnp.where(near, GROUP, num_micro)
     prep_at = jnp.where(me == 0, num_micro, 0)
 
     def slot(t, carry):
@@ -254,7 +263,7 @@
         does_f = t < num_micro
         does_b = (i >= 0) & (i < num_micro)
         does_w = k >= 0
-        which = lax.rem(k + 4, 2)
+        which = lax.rem(k + 2 * num_micro, 2)
 
         @pl.when(t == prep_at)
         def _():
@@ -295,21 +304,46 @@
                 ship_bwd(m)
             each(i, step)
 
+        @pl.when(does_b & (near == False))
+        def _():
+            store_e(i).start()
+
+            @pl.when(i > 0)
+            def _():
+                store_e(i - 1).wait()
+
+        @pl.when((i == num_micro) & (near == False))
+        def _():
+            store_e(num_micro - 1).wait()
+            load_e(0).start()
+
+        @pl.when(does_w & (which == 0) & near)
+        def _():
+            wgt(k, 0, True)
+
+        @pl.when(does_w & (which == 0) & (near == False))
+        def _():
+            @pl.when(k + 2 < num_micro)
+            def _():
+                load_e(k + 2).start()
+            load_e(k).wait()
+            wgt(k, 0, False)
+
+        @pl.when(does_w & (which == 1))
+        def _():
+            wgt(k, 1, True)
+
         for pick in range(2):
-            @pl.when(does_w & (which == pick))
+            @pl.when((k >= num_micro - 4) & (which == pick))
             def _(pick=pick):
-                for piece in wgt(k, pick):
-                    piece()
+                result(k, pick).start()
 
         return carry
 
     lax.fori_loop(0, num_micro + warm + lag, slot, 0)
 
-    outs = [pltpu.make_async_copy(acc.at[0], ga_out, o_sem.at[0]),
-            pltpu.make_async_copy(acc.at[1], gb_out, o_sem.at[1]),
-            pltpu.make_async_copy(lossv, loss_out, o_sem.at[2])]
-    for copy in outs:
-        copy.start()
+    loss_copy = pltpu.make_async_copy(lossv, loss_out, e_in.at[0])
+    loss_copy.start()
 
     @pl.when(me > 0)
     def _():
@@ -320,8 +354,9 @@
             return c
         lax.fori_loop((num_micro - SENDS) * HALVES, num_micro * HALVES, drain, 0)
 
-    for copy in outs:
-        copy.wait()
+    loss_copy.wait()
+    for k in range(4):
+        result(k, k % 2).wait()
 
 
 def solution(mesh):
@@ -333,11 +368,11 @@
         ring = min(RING, num_micro)
         any_spec = pl.BlockSpec(memory_space=pl.ANY)
         dma = pltpu.SemaphoreType.DMA
-        grad_a, grad_bt, loss = pl.pallas_call(
+        grad_a, grad_bt, loss, _ = pl.pallas_call(
             functools.partial(kernel, stages, num_micro, ring),
-            out_shape=(jax.ShapeDtypeStruct((2, model, hidden), F32), jax.ShapeDtypeStruct((2, model, hidden), F32), jax.ShapeDtypeStruct((8, 128), F32)),
+            out_shape=(jax.ShapeDtypeStruct((2, model, hidden), F32), jax.ShapeDtypeStruct((2, model, hidden), F32), jax.ShapeDtypeStruct((8, 128), F32), jax.ShapeDtypeStruct((2, num_micro, tokens, hidden), BF16)),
             in_specs=[any_spec] * 4,
-            out_specs=(any_spec,) * 3,
+            out_specs=(any_spec,) * 4,
             scratch_shapes=[
                 pltpu.VMEM((2, model, hidden), BF16),
                 pltpu.VMEM((2, hidden, model), BF16),
@@ -347,6 +382,7 @@
                 pltpu.VMEM((2, num_micro, tokens, hidden), BF16),
                 pltpu.VMEM((2, num_micro, tokens, model), BF16),
                 pltpu.VMEM((2, ring, tokens, hidden), BF16),
+                pltpu.VMEM((2, GROUP, tokens, hidden), BF16),
                 pltpu.VMEM((2, 2, model, hidden), F32),
                 pltpu.VMEM((2, tokens, hidden), BF16),
                 pltpu.VMEM((2, tokens, hidden), BF16),
@@ -356,7 +392,7 @@
                 pltpu.VMEM((model, GROUP * tokens), BF16),
                 pltpu.VMEM((8, 128), F32),
                 dma((num_micro * HALVES,)), dma((num_micro * HALVES,)), dma((num_micro * HALVES,)), dma((SENDS * HALVES,)),
-                dma((2,)), dma(()), dma(()), dma((3,)),
+                dma((2,)), dma(()), dma(()), dma((2, 2)), dma((ring,)), dma((2,)),
             ],
             compiler_params=pltpu.CompilerParams(collective_id=0, has_side_effects=True, vmem_limit_bytes=67043328),
         )(micro_in, targets, w_in[0], w_out[0])

time: 328 us -> 328 us (level)
  no operation moved by 1% of the time
where the time goes in v3:
time: 328 us
  Pallas kernels  316 us (96%)
  local copies, waits for them, and re-layouts  10.2 us (3%)
    pallas_call x1, Pallas kernels, per_device(): pl.pallas_call(functools.partial(kernel, stages, num_micro, ring), out_sh...  316 us
    unnamed x2, local copies, waits for them, and re-layouts  10.2 us

profile of v3, /device:TPU:96, one launch (start us, length us, event | category | flops | bytes accessed | tf_op | source)
XLA Modules:
  0.0 327.7 jit_solution(1537771954078860423)
XLA Ops:
  0.6 315.7 %shard_map.67 = (f32[2,512,1024]{2,1,0:T(8,128)}, f32[2,512,1024]{2,1,0:T(8,128)}, f32[8,128]{1,0:T(8,128)}, bf16[2,32,128,1024]{3,2,1,0:T(8,128)(2,1)}) custom-call(bf16[32,128,512]{2,1,0:T(8,128)(2,1)} %x_hbm.1, bf16[32,128,512]{2,1,0:T(8,128)(2,1)} %t_hbm.1, bf16[2,512,1024]{2,1,0:T(8,128)(2,1)} %bitcast.9, bf16[2,1024,512]{2,1,0:T(8,128)(2,1)} %bitcast.10), custom_call_target="tpu_custom_call" | custom-call | tf_op jit(solution)/shard_map/pallas_call | solution.py:371
  316.3 1.3 reduce_sum.9
  317.6 5.4 %copy.7 = f32[1,2,1024,512]{3,2,1,0:T(8,128)} copy(f32[1,2,1024,512]{2,3,1,0:T(8,128)} %bitcast.8) | data formatting | bytes 8388608
  322.9 4.8 %copy.9 = f32[1,2,512,1024]{3,2,1,0:T(8,128)} copy(f32[1,2,512,1024]{3,2,1,0:T(8,128)} %bitcast.7) | data formatting | bytes 8388608

commit v4 on v3

--- a/solution.py
+++ b/solution.py
@@ -15,7 +15,7 @@
 RING = 8
 SENDS = 4
 PAIR_SLACK = 3
-CHIP_SLACK = 7
+CHIP_SLACK = 5
 NEAR = 8
 HALVES = 2
 
@@ -296,7 +296,13 @@
             each(i, ship_bwd)
             each(t, ship_fwd)
 
-        @pl.when(does_b & (t >= num_micro))
+        @pl.when(does_b & (t >= num_micro) & near)
+        def _():
+            each(i, wait_bwd)
+            run(bwd_steps(i, slice(None), tokens))
+            each(i, ship_bwd)
+
+        @pl.when(does_b & (t >= num_micro) & (near == False))
         def _():
             def step(m):
                 wait_bwd(m)
@@ -357,6 +363,24 @@
     loss_copy.wait()
     for k in range(4):
         result(k, k % 2).wait()
+
+
+def finish(ga, gbt, loss, ga_out, gb_out, loss_out):
+    ga_out[...] = ga[...]
+    gb_out[0] = gbt[0].T
+    loss_out[0] = jnp.sum(loss[...])
+
+
+def write_results(grad_a, grad_bt, loss):
+    layers, model, hidden = grad_a.shape
+    rows, cols = model // 4, hidden // 4
+    return pl.pallas_call(
+        finish,
+        grid=(layers, 4),
+        in_specs=[pl.BlockSpec((1, rows, hidden), lambda l, b: (l, b, 0)), pl.BlockSpec((1, model, cols), lambda l, b: (l, 0, b)), pl.BlockSpec(loss.shape, lambda l, b: (0, 0))],
+        out_specs=(pl.BlockSpec((1, rows, hidden), lambda l, b: (l, b, 0)), pl.BlockSpec((1, cols, model), lambda l, b: (l, b, 0)), pl.BlockSpec(memory_space=pltpu.SMEM)),
+        out_shape=(jax.ShapeDtypeStruct((layers, model, hidden), F32), jax.ShapeDtypeStruct((layers, hidden, model), F32), jax.ShapeDtypeStruct((1,), F32)),
+    )(grad_a, grad_bt, loss)
 
 
 def solution(mesh):
@@ -396,6 +420,7 @@
             ],
             compiler_params=pltpu.CompilerParams(collective_id=0, has_side_effects=True, vmem_limit_bytes=67043328),
         )(micro_in, targets, w_in[0], w_out[0])
-        return grad_a[None], jnp.swapaxes(grad_bt, 1, 2)[None], jnp.sum(loss).reshape(1)
+        grad_a, grad_b, total = write_results(grad_a, grad_bt, loss)
+        return grad_a[None], grad_b[None], total
 
     return jax.shard_map(per_device, mesh=mesh, in_specs=(P('data'), P('data'), P('stage'), P('stage')), out_specs=(P(('data', 'stage')), P(('data', 'stage')), P('data')), check_vma=False)

time: 328 us -> 302 us (0.921)
  Pallas kernels: 316 us -> 301 us
  local copies, waits for them, and re-layouts: 10.2 us -> 0 us
    pallas_call x1, Pallas kernels: 316 us -> 292 us  [per_device(): pl.pallas_call(functools.partial(kernel, stages, num_micro, ring), out_sh...]
    unnamed x2 -> x0, local copies, waits for them, and re-layouts: 10.2 us -> none
    pallas_call x0 -> x1, Pallas kernels: none -> 9.25 us  [write_results(): pl.pallas_call(finish, grid=(layers, 4), in_specs=[pl.BlockSpec((1, rows,...]
where the time goes in v4:
time: 302 us
  Pallas kernels  301 us (100%)
    pallas_call x1, Pallas kernels, per_device(): pl.pallas_call(functools.partial(kernel, stages, num_micro, ring), out_sh...  292 us
    pallas_call x1, Pallas kernels, write_results(): pl.pallas_call(finish, grid=(layers, 4), in_specs=[pl.BlockSpec((1, rows,...  9.25 us

profile of v4, /device:TPU:96, one launch (start us, length us, event | category | flops | bytes accessed | tf_op | source)
XLA Modules:
  0.0 302.0 jit_solution(5232249938742026685)
XLA Ops:
  0.6 292.1 %shard_map.67 = (f32[2,512,1024]{2,1,0:T(8,128)}, f32[2,512,1024]{2,1,0:T(8,128)}, f32[8,128]{1,0:T(8,128)}, bf16[2,32,128,1024]{3,2,1,0:T(8,128)(2,1)}) custom-call(bf16[32,128,512]{2,1,0:T(8,128)(2,1)} %x_hbm.1, bf16[32,128,512]{2,1,0:T(8,128)(2,1)} %t_hbm.1, bf16[2,512,1024]{2,1,0:T(8,128)(2,1)} %bitcast.4, bf16[2,1024,512]{2,1,0:T(8,128)(2,1)} %bitcast.5), custom_call_target="tpu_custom_call" | custom-call | tf_op jit(solution)/shard_map/pallas_call | solution.py:395
  292.8 9.2 %shard_map.68 = (f32[2,512,1024]{2,1,0:T(8,128)}, f32[2,1024,512]{2,1,0:T(8,128)}, f32[1]{0:T(128)}) custom-call(f32[2,512,1024]{2,1,0:T(8,128)} %get-tuple-element.9.ga, f32[2,512,1024]{2,1,0:T(8,128)} %get-tuple-element.10.gbt, f32[8,128]{1,0:T(8,128)} %get-tuple-element.11.loss), custom_call_target="tpu_custom_call" | custom-call | tf_op jit(solution)/shard_map/pallas_call | solution.py:377

commit v5 on v4

v5 whole, which is shorter than its diff:
```python
import functools
import jax
import jax.numpy as jnp
from jax import lax
from jax.experimental import pallas as pl
from jax.experimental.pallas import tpu as pltpu
from jax.sharding import PartitionSpec as P

BF16 = jnp.bfloat16
F32 = jnp.float32
C0 = 0.7978845608028654
C1 = 0.044715 * C0
GROUP = 4
LANES = 128
RING = 8
SENDS = 4
PAIR_SLACK = 4
CHIP_SLACK = 5
NEAR = 8
HALVES = 2
SPLIT = 2


def gelu(x):
    return x * (0.5 + 0.5 * jnp.tanh(x * (C0 + C1 * (x * x))))


def gelu_pair(x):
    sq = x * x
    t = jnp.tanh(x * (C0 + C1 * sq))
    cdf = 0.5 + 0.5 * t
    slope = cdf + (x * (0.5 * C0 + 1.5 * C1 * sq)) * (1.0 - t * t)
    return x * cdf, slope


def pairs(width):
    return [(c, c + 2) for c in range(0, width // LANES, 2)]


def join(parts):
    return jnp.concatenate(list(parts), axis=-1)


def kernel(stages, num_micro, ring, x_hbm, t_hbm, wa_hbm, wb_hbm, ga_out, gb_out, loss_out, e_hbm,
           wa, wb, wat, wbt, hh, uu, gg, ee, es, acc, act, et, hm, gm, gout, xt, lossv,
           f_recv, f_send, g_recv, g_send, w_sem, l_recv, l_send, o_sem, e_out, e_in):
    tokens = hh.shape[-2]
    model, hidden = hh.shape[-3] * LANES, uu.shape[-3] * LANES
    mcols, hcols = range(model // LANES), range(hidden // LANES)
    me = lax.axis_index('stage')
    last = stages - 1
    is_last = me == last
    loss_scale = 1.0 / (num_micro * tokens * model)

    half = tokens // HALVES

    def part(m):
        return m // HALVES, pl.ds(pl.multiple_of(lax.rem(m, HALVES) * half, half), half)

    def lanes(c):
        return pl.ds(c * LANES, LANES)

    for l in range(2):
        for c in hcols:
            pltpu.make_async_copy(wa_hbm.at[l, :, lanes(c)], wa.at[l, c], w_sem.at[0]).start()
        for c in mcols:
            pltpu.make_async_copy(wb_hbm.at[l, :, lanes(c)], wb.at[l, c], w_sem.at[1]).start()

    @pl.when(me == 0)
    def _():
        def load(m, c):
            j, rows = part(m)
            for col in mcols:
                pltpu.make_async_copy(x_hbm.at[j, rows, lanes(col)], hh.at[0, j, col, rows], f_recv.at[m]).start()
            return c
        lax.fori_loop(0, num_micro * HALVES, load, 0)

    @pl.when(is_last)
    def _():
        def load(m, c):
            j, rows = part(m)
            for col in mcols:
                pltpu.make_async_copy(t_hbm.at[j, rows, lanes(col)], gg.at[1, j, col, rows], g_recv.at[m]).start()
            return c
        lax.fori_loop(0, num_micro * HALVES, load, 0)
        lossv[...] = jnp.zeros_like(lossv)

    barrier = pltpu.get_barrier_semaphore()

    @pl.when(me > 0)
    def _():
        pl.semaphore_signal(barrier, inc=1, device_id={'stage': me - 1}, device_id_type=pl.DeviceIdType.MESH)

    @pl.when(me < last)
    def _():
        pl.semaphore_signal(barrier, inc=1, device_id={'stage': me + 1}, device_id_type=pl.DeviceIdType.MESH)

    pl.semaphore_wait(barrier, jnp.where((me == 0) | is_last, 1, 2))

    pltpu.make_async_copy(wa, wa, w_sem.at[0]).wait()
    pltpu.make_async_copy(wb, wb, w_sem.at[1]).wait()

    def send_fwd(m):
        j, rows = part(m)
        return pltpu.make_async_remote_copy(
            src_ref=gg.at[0, j, :, rows], dst_ref=hh.at[0, j, :, rows], send_sem=f_send.at[m], recv_sem=f_recv.at[m],
            device_id={'stage': jnp.minimum(me + 1, last)}, device_id_type=pl.DeviceIdType.MESH)

    def send_bwd(m):
        i, rows = part(m)
        return pltpu.make_async_remote_copy(
            src_ref=gout.at[lax.rem(i, SENDS), :, rows], dst_ref=gg.at[1, i, :, rows],
            send_sem=g_send.at[lax.rem(m, SENDS * HALVES)], recv_sem=g_recv.at[m],
            device_id={'stage': jnp.maximum(me - 1, 0)}, device_id_type=pl.DeviceIdType.MESH)

    def send_loss():
        return pltpu.make_async_remote_copy(
            src_ref=lossv, dst_ref=lossv, send_sem=l_send, recv_sem=l_recv,
            device_id={'stage': jnp.maximum(me - 1, 0)}, device_id_type=pl.DeviceIdType.MESH)

    def prepare():
        for l in range(2):
            for r in mcols:
                for c in hcols:
                    wat[l, r, lanes(c)] = wa[l, c, lanes(r)].T
                    wbt[l, c, lanes(r)] = wb[l, r, lanes(c)].T

        def clear(r, c):
            rows = pl.ds(pl.multiple_of(r * 8, 8), 8)
            for l in range(2):
                for col in hcols:
                    for which in range(2):
                        acc[which, l, col, rows] = jnp.zeros((8, LANES), F32)
            return c
        lax.fori_loop(0, model // 8, clear, 0)

    def fwd_steps(j, rows, n):
        def up(l, cols):
            h = join(hh[0, j, c, rows] if l == 0 else hm[c, :n] for c in mcols)
            pre = jnp.dot(h, join(wa[l, c] for c in range(*cols)), preferred_element_type=F32).astype(BF16)
            val = gelu(pre.astype(F32)).astype(BF16)
            for at, c in enumerate(range(*cols)):
                uu[l, j, c, rows] = pre[:, at * LANES:(at + 1) * LANES]
                act[l, c, :n] = val[:, at * LANES:(at + 1) * LANES]

        def down(l, cols):
            branch = jnp.dot(join(act[l, c, :n] for c in hcols), join(wb[l, c] for c in range(*cols)), preferred_element_type=F32)
            for at, c in enumerate(range(*cols)):
                h = hh[0, j, c, rows] if l == 0 else hm[c, :n]
                out = (h.astype(F32) + branch[:, at * LANES:(at + 1) * LANES]).astype(BF16)
                if l == 0:
                    hm[c, :n] = out
                    hh[1, j, c, rows] = out
                else:
                    gg[0, j, c, rows] = out

        steps = []
        for l in range(2):
            steps.append([functools.partial(up, l, c) for c in pairs(hidden)])
            steps.append([functools.partial(down, l, c) for c in pairs(model)])
        return steps

    def bwd_steps(i, rows, n):
        slot = lax.rem(i, ring)
        out_slot = lax.rem(i, SENDS)

        def up(l, cols):
            g = join(gg[1, i, c, rows] if l == 1 else gm[c, :n] for c in mcols)
            grad_act = jnp.dot(g, join(wbt[l, c] for c in range(*cols)), preferred_element_type=F32)
            for at, c in enumerate(range(*cols)):
                val, slope = gelu_pair(uu[l, i, c, rows].astype(F32))
                e = (slope * grad_act[:, at * LANES:(at + 1) * LANES]).astype(BF16)
                et[l, c, :n] = e
                ee[l, slot, c, rows] = e
                uu[l, i, c, rows] = val.astype(BF16)

        def down(l, cols):
            back = jnp.dot(join(et[l, c, :n] for c in hcols), join(wat[l, c] for c in range(*cols)), preferred_element_type=F32)
            for at, c in enumerate(range(*cols)):
                g = gg[1, i, c, rows] if l == 1 else gm[c, :n]
                out = (g.astype(F32) + back[:, at * LANES:(at + 1) * LANES]).astype(BF16)
                if l == 1:
                    gm[c, :n] = out
                    gg[0, i, c, rows] = out
                else:
                    gout[out_slot, c, rows] = out

        steps = []
        for l in (1, 0):
            steps.append([functools.partial(up, l, c) for c in pairs(hidden)])
            steps.append([functools.partial(down, l, c) for c in pairs(model)])
        return steps

    def store_e(i):
        slot = lax.rem(i, ring)
        return pltpu.make_async_copy(ee.at[:, slot], e_hbm.at[:, i], e_out.at[slot])

    def load_e(k):
        l, first, buf = lax.rem(k // 2, 2), (k // 4) * GROUP, lax.rem(k // 2, 2)
        return pltpu.make_async_copy(e_hbm.at[l, pl.ds(first, GROUP)], es.at[buf], e_in.at[buf])

    def result(k, pick):
        l = lax.rem(k // 2, 2)
        return pltpu.make_async_copy(acc.at[pick, l], (ga_out, gb_out)[pick].at[l], o_sem.at[pick, l])

    def wgt(k, pick, direct):
        l = lax.rem(k // 2, 2)
        first = (k // 4) * GROUP
        src = hh if pick == 0 else gg
        for q in range(GROUP):
            for c in mcols:
                xt[q, lanes(c)] = src[l, first + q, c].T

        def column(c):
            if pick == 0 and direct:
                y = ee[l, pl.ds(lax.rem(first, ring), GROUP), c]
            elif pick == 0:
                y = es[lax.rem(k // 2, 2), :, c]
            else:
                y = uu[l, pl.ds(first, GROUP), c]
            return y.reshape(GROUP * tokens, LANES)

        for cols in pairs(hidden):
            part_sum = jnp.dot(join(xt[q] for q in range(GROUP)), join(column(c) for c in range(*cols)), preferred_element_type=F32)
            for at, c in enumerate(range(*cols)):
                acc[pick, l, c] += part_sum[:, at * LANES:(at + 1) * LANES]

    def run(*lists):
        for steps in lists:
            for pieces in steps:
                for piece in pieces:
                    piece()

    def wait_fwd(m):
        j, rows = part(m)
        pltpu.make_async_copy(hh.at[0, j, :, rows], hh.at[0, j, :, rows], f_recv.at[m]).wait()

    def wait_bwd(m):
        i, rows = part(m)

        @pl.when(is_last == False)
        def _():
            pltpu.make_async_copy(gg.at[1, i, :, rows], gg.at[1, i, :, rows], g_recv.at[m]).wait()
            send_fwd(m).wait_send()

        @pl.when((me > 0) & (m >= SENDS * HALVES))
        def _():
            send_bwd(m - SENDS * HALVES).wait_send()

    def ship_fwd(m):
        j, rows = part(m)

        @pl.when(is_last == False)
        def _():
            send_fwd(m).start()

        @pl.when(is_last)
        def _():
            pltpu.make_async_copy(gg.at[1, j, :, rows], gg.at[1, j, :, rows], g_recv.at[m]).wait()
            total = jnp.zeros((8, LANES), F32)
            for c in mcols:
                res = gg[0, j, c, rows].astype(F32) - gg[1, j, c, rows].astype(F32)
                gg[1, j, c, rows] = (res * loss_scale).astype(BF16)
                total = total + jnp.sum((res * res).reshape(half // 8, 8, LANES), axis=0)
            lossv[...] += total * (0.5 * loss_scale)

    def ship_bwd(m):
        @pl.when(me > 0)
        def _():
            send_bwd(m).start()

    def each(j, body):
        def step(b, c):
            body(j * HALVES + b)
            return c
        lax.fori_loop(0, HALVES, step, 0)

    warm = jnp.minimum(num_micro, 1 + PAIR_SLACK * ((last - me + 1) // 2) + CHIP_SLACK * ((last - me) // 2))
    near = me < NEAR
    lag = jnp.where(near, GROUP, num_micro)
    prep_at = jnp.where(me == 0, num_micro, 0)

    def slot(t, carry):
        i = t - warm
        k = i - lag
        does_f = t < num_micro
        does_b = (i >= 0) & (i < num_micro)
        does_w = k >= 0
        which = lax.rem(k + 2 * num_micro, 2)

        @pl.when(t == prep_at)
        def _():
            prepare()

        @pl.when(i == num_micro - 1)
        def _():
            @pl.when(is_last == False)
            def _():
                pltpu.make_async_copy(lossv, lossv, l_recv).wait()

            @pl.when(me > 0)
            def _():
                send_loss().start()

        @pl.when(does_f & (i < 0))
        def _():
            def step(m):
                wait_fwd(m)
                run(fwd_steps(*part(m), half))
                ship_fwd(m)
            each(t, step)

        @pl.when(does_f & (i >= 0))
        def _():
            rows = slice(None)
            each(t, wait_fwd)
            each(i, wait_bwd)
            run(fwd_steps(t, rows, tokens), bwd_steps(i, rows, tokens))
            each(i, ship_bwd)
            each(t, ship_fwd)

        @pl.when(does_b & (t >= num_micro) & near)
        def _():
            each(i, wait_bwd)
            run(bwd_steps(i, slice(None), tokens))
            each(i, ship_bwd)

        @pl.when(does_b & (t >= num_micro) & (near == False))
        def _():
            def step(m):
                wait_bwd(m)
                run(bwd_steps(*part(m), half))
                ship_bwd(m)
            each(i, step)

        @pl.when(does_b & (near == False))
        def _():
            store_e(i).start()

            @pl.when(i > 0)
            def _():
                store_e(i - 1).wait()

        @pl.when((i == num_micro) & (near == False))
        def _():
            store_e(num_micro - 1).wait()
            load_e(0).start()

        @pl.when(does_w & (which == 0) & near)
        def _():
            wgt(k, 0, True)

        @pl.when(does_w & (which == 0) & (near == False))
        def _():
            @pl.when(k + 2 < num_micro)
            def _():
                load_e(k + 2).start()
            load_e(k).wait()
            wgt(k, 0, False)

        @pl.when(does_w & (which == 1))
        def _():
            wgt(k, 1, True)

        for pick in range(2):
            @pl.when((k >= num_micro - 4) & (which == pick))
            def _(pick=pick):
                result(k, pick).start()

        return carry

    lax.fori_loop(0, num_micro + warm + lag, slot, 0)

    loss_copy = pltpu.make_async_copy(lossv, loss_out, e_in.at[0])
    loss_copy.start()

    @pl.when(me > 0)
    def _():
        send_loss().wait_send()

        def drain(m, c):
            send_bwd(m).wait_send()
            return c
        lax.fori_loop((num_micro - SENDS) * HALVES, num_micro * HALVES, drain, 0)

    loss_copy.wait()
    for k in range(4):
        result(k, k % 2).wait()


def finish(ga, gbt, loss, ga_out, gb_out, loss_out):
    for c in range(ga.shape[1]):
        ga_out[0, :, c * LANES:(c + 1) * LANES] = ga[0, c]
    for c in range(gbt.shape[1]):
        gb_out[0, c * LANES:(c + 1) * LANES] = gbt[0, c].T
    loss_out[0] = jnp.sum(loss[...])


def write_results(grad_a, grad_bt, loss):
    layers, cols, model, _ = grad_a.shape
    hidden = cols * LANES
    rows = model // SPLIT
    return pl.pallas_call(
        finish,
        grid=(layers, SPLIT),
        in_specs=[pl.BlockSpec((1, cols, rows, LANES), lambda l, b: (l, 0, b, 0)), pl.BlockSpec((1, cols // SPLIT, model, LANES), lambda l, b: (l, b, 0, 0)), pl.BlockSpec(loss.shape, lambda l, b: (0, 0))],
        out_specs=(pl.BlockSpec((1, rows, hidden), lambda l, b: (l, b, 0)), pl.BlockSpec((1, hidden // SPLIT, model), lambda l, b: (l, b, 0)), pl.BlockSpec(memory_space=pltpu.SMEM)),
        out_shape=(jax.ShapeDtypeStruct((layers, model, hidden), F32), jax.ShapeDtypeStruct((layers, hidden, model), F32), jax.ShapeDtypeStruct((1,), F32)),
    )(grad_a, grad_bt, loss)


def solution(mesh):
    stages = mesh.shape['stage']

    def per_device(micro_in, targets, w_in, w_out):
        num_micro, tokens, model = micro_in.shape
        hidden = w_in.shape[-1]
        ring = min(RING, num_micro)
        any_spec = pl.BlockSpec(memory_space=pl.ANY)
        dma = pltpu.SemaphoreType.DMA
        mcols, hcols = model // LANES, hidden // LANES
        grad = jax.ShapeDtypeStruct((2, hcols, model, LANES), F32)
        grad_a, grad_bt, loss, _ = pl.pallas_call(
            functools.partial(kernel, stages, num_micro, ring),
            out_shape=(grad, grad, jax.ShapeDtypeStruct((8, 128), F32), jax.ShapeDtypeStruct((2, num_micro, hcols, tokens, LANES), BF16)),
            in_specs=[any_spec] * 4,
            out_specs=(any_spec,) * 4,
            scratch_shapes=[
                pltpu.VMEM((2, hcols, model, LANES), BF16),
                pltpu.VMEM((2, mcols, hidden, LANES), BF16),
                pltpu.VMEM((2, mcols, hidden, LANES), BF16),
                pltpu.VMEM((2, hcols, model, LANES), BF16),
                pltpu.VMEM((2, num_micro, mcols, tokens, LANES), BF16),
                pltpu.VMEM((2, num_micro, hcols, tokens, LANES), BF16),
                pltpu.VMEM((2, num_micro, mcols, tokens, LANES), BF16),
                pltpu.VMEM((2, ring, hcols, tokens, LANES), BF16),
                pltpu.VMEM((2, GROUP, hcols, tokens, LANES), BF16),
                pltpu.VMEM((2, 2, hcols, model, LANES), F32),
                pltpu.VMEM((2, hcols, tokens, LANES), BF16),
                pltpu.VMEM((2, hcols, tokens, LANES), BF16),
                pltpu.VMEM((mcols, tokens, LANES), BF16),
                pltpu.VMEM((mcols, tokens, LANES), BF16),
                pltpu.VMEM((SENDS, mcols, tokens, LANES), BF16),
                pltpu.VMEM((GROUP * tokens // LANES, model, LANES), BF16),
                pltpu.VMEM((8, 128), F32),
                dma((num_micro * HALVES,)), dma((num_micro * HALVES,)), dma((num_micro * HALVES,)), dma((SENDS * HALVES,)),
                dma((2,)), dma(()), dma(()), dma((2, 2)), dma((ring,)), dma((2,)),
            ],
            compiler_params=pltpu.CompilerParams(collective_id=0, has_side_effects=True, vmem_limit_bytes=67043328),
        )(micro_in, targets, w_in[0], w_out[0])
        grad_a, grad_b, total = write_results(grad_a, grad_bt, loss)
        return grad_a[None], grad_b[None], total

    return jax.shard_map(per_device, mesh=mesh, in_specs=(P('data'), P('data'), P('stage'), P('stage')), out_specs=(P(('data', 'stage')), P(('data', 'stage')), P('data')), check_vma=False)
```

time: 302 us -> 314 us (1.040)
  Pallas kernels: 301 us -> 313 us
    pallas_call x1, Pallas kernels: 292 us -> 306 us  [per_device(): pl.pallas_call(functools.partial(kernel, stages, num_micro, ring), out_sh...]
where the time goes in v5:
time: 314 us
  Pallas kernels  313 us (100%)
    pallas_call x1, Pallas kernels, per_device(): pl.pallas_call(functools.partial(kernel, stages, num_micro, ring), out_sh...  306 us
    pallas_call x1, Pallas kernels, write_results(): pl.pallas_call(finish, grid=(layers, SPLIT), in_specs=[pl.BlockSpec((1, c...  7.47 us

profile of v5, /device:TPU:96, one launch (start us, length us, event | category | flops | bytes accessed | tf_op | source)
XLA Modules:
  0.0 314.0 jit_solution(13414825561425687381)
XLA Ops:
  0.6 305.9 %shard_map.67 = (f32[2,8,512,128]{3,2,1,0:T(8,128)}, f32[2,8,512,128]{3,2,1,0:T(8,128)}, f32[8,128]{1,0:T(8,128)}, bf16[2,32,8,128,128]{4,3,2,1,0:T(8,128)(2,1)}) custom-call(bf16[32,128,512]{2,1,0:T(8,128)(2,1)} %x_hbm.1, bf16[32,128,512]{2,1,0:T(8,128)(2,1)} %t_hbm.1, bf16[2,512,1024]{2,1,0:T(8,128)(2,1)} %bitcast.4, bf16[2,1024,512]{2,1,0:T(8,128)(2,1)} %bitcast.5), custom_call_target="tpu_custom_call" | custom-call | tf_op jit(solution)/shard_map/pallas_call | solution.py:423
  306.5 7.5 %shard_map.68 = (f32[2,512,1024]{2,1,0:T(8,128)}, f32[2,1024,512]{2,1,0:T(8,128)}, f32[1]{0:T(128)}) custom-call(f32[2,8,512,128]{3,2,1,0:T(8,128)} %get-tuple-element.9.ga, f32[2,8,512,128]{3,2,1,0:T(8,128)} %get-tuple-element.10.gbt, f32[8,128]{1,0:T(8,128)} %get-tuple-element.11.loss), custom_call_target="tpu_custom_call" | custom-call | tf_op jit(solution)/shard_map/pallas_call | solution.py:403

commit v6 on v4

--- a/solution.py
+++ b/solution.py
@@ -14,10 +14,12 @@
 TILE = 256
 RING = 8
 SENDS = 4
-PAIR_SLACK = 3
+PAIR_SLACK = 2
 CHIP_SLACK = 5
 NEAR = 8
 HALVES = 2
+LATE = 4
+SPLIT = 2
 
 
 def gelu(x):
@@ -252,7 +254,7 @@
             return c
         lax.fori_loop(0, HALVES, step, 0)
 
-    warm = jnp.minimum(num_micro, 1 + PAIR_SLACK * ((last - me + 1) // 2) + CHIP_SLACK * ((last - me) // 2))
+    warm = jnp.minimum(num_micro, PAIR_SLACK * ((last - me + 1) // 2) + CHIP_SLACK * ((last - me) // 2))
     near = me < NEAR
     lag = jnp.where(near, GROUP, num_micro)
     prep_at = jnp.where(me == 0, num_micro, 0)
@@ -269,17 +271,11 @@
         def _():
             prepare()
 
-        @pl.when(i == num_micro - 1)
-        def _():
-            @pl.when(is_last == False)
-            def _():
-                pltpu.make_async_copy(lossv, lossv, l_recv).wait()
-
-            @pl.when(me > 0)
-            def _():
-                send_loss().start()
-
-        @pl.when(does_f & (i < 0))
+        f_split = (i < 0) & (me < stages - LATE)
+        b_split = (t >= num_micro) & (near == False) & (me < stages - LATE)
+        whole = slice(None)
+
+        @pl.when(does_f & f_split)
         def _():
             def step(m):
                 wait_fwd(m)
@@ -287,22 +283,23 @@
                 ship_fwd(m)
             each(t, step)
 
-        @pl.when(does_f & (i >= 0))
-        def _():
-            rows = slice(None)
+        @pl.when(does_f & (f_split == False))
+        def _():
             each(t, wait_fwd)
-            each(i, wait_bwd)
-            run(fwd_steps(t, rows, tokens), bwd_steps(i, rows, tokens))
-            each(i, ship_bwd)
+            run(fwd_steps(t, whole, tokens))
             each(t, ship_fwd)
 
-        @pl.when(does_b & (t >= num_micro) & near)
-        def _():
-            each(i, wait_bwd)
-            run(bwd_steps(i, slice(None), tokens))
-            each(i, ship_bwd)
-
-        @pl.when(does_b & (t >= num_micro) & (near == False))
+        @pl.when(i == num_micro - 1)
+        def _():
+            @pl.when(is_last == False)
+            def _():
+                pltpu.make_async_copy(lossv, lossv, l_recv).wait()
+
+            @pl.when(me > 0)
+            def _():
+                send_loss().start()
+
+        @pl.when(does_b & b_split)
         def _():
             def step(m):
                 wait_bwd(m)
@@ -310,6 +307,12 @@
                 ship_bwd(m)
             each(i, step)
 
+        @pl.when(does_b & (b_split == False))
+        def _():
+            each(i, wait_bwd)
+            run(bwd_steps(i, whole, tokens))
+            each(i, ship_bwd)
+
         @pl.when(does_b & (near == False))
         def _():
             store_e(i).start()
@@ -373,10 +376,10 @@
 
 def write_results(grad_a, grad_bt, loss):
     layers, model, hidden = grad_a.shape
-    rows, cols = model // 4, hidden // 4
+    rows, cols = model // SPLIT, hidden // SPLIT
     return pl.pallas_call(
         finish,
-        grid=(layers, 4),
+        grid=(layers, SPLIT),
         in_specs=[pl.BlockSpec((1, rows, hidden), lambda l, b: (l, b, 0)), pl.BlockSpec((1, model, cols), lambda l, b: (l, 0, b)), pl.BlockSpec(loss.shape, lambda l, b: (0, 0))],
         out_specs=(pl.BlockSpec((1, rows, hidden), lambda l, b: (l, b, 0)), pl.BlockSpec((1, cols, model), lambda l, b: (l, b, 0)), pl.BlockSpec(memory_space=pltpu.SMEM)),
         out_shape=(jax.ShapeDtypeStruct((layers, model, hidden), F32), jax.ShapeDtypeStruct((layers, hidden, model), F32), jax.ShapeDtypeStruct((1,), F32)),

time: 302 us -> 296 us (0.980)
  Pallas kernels: 301 us -> 295 us
    pallas_call x1, Pallas kernels: 292 us -> 287 us  [per_device(): pl.pallas_call(functools.partial(kernel, stages, num_micro, ring), out_sh...]
where the time goes in v6:
time: 296 us
  Pallas kernels  295 us (100%)
    pallas_call x1, Pallas kernels, per_device(): pl.pallas_call(functools.partial(kernel, stages, num_micro, ring), out_sh...  287 us
    pallas_call x1, Pallas kernels, write_results(): pl.pallas_call(finish, grid=(layers, SPLIT), in_specs=[pl.BlockSpec((1, r...  7.42 us

profile of v6, /device:TPU:96, one launch (start us, length us, event | category | flops | bytes accessed | tf_op | source)
XLA Modules:
  0.0 295.5 jit_solution(4144877475367542733)
XLA Ops:
  0.6 287.5 %shard_map.67 = (f32[2,512,1024]{2,1,0:T(8,128)}, f32[2,512,1024]{2,1,0:T(8,128)}, f32[8,128]{1,0:T(8,128)}, bf16[2,32,128,1024]{3,2,1,0:T(8,128)(2,1)}) custom-call(bf16[32,128,512]{2,1,0:T(8,128)(2,1)} %x_hbm.1, bf16[32,128,512]{2,1,0:T(8,128)(2,1)} %t_hbm.1, bf16[2,512,1024]{2,1,0:T(8,128)(2,1)} %bitcast.4, bf16[2,1024,512]{2,1,0:T(8,128)(2,1)} %bitcast.5), custom_call_target="tpu_custom_call" | custom-call | tf_op jit(solution)/shard_map/pallas_call | solution.py:398
  288.1 7.4 %shard_map.68 = (f32[2,512,1024]{2,1,0:T(8,128)}, f32[2,1024,512]{2,1,0:T(8,128)}, f32[1]{0:T(128)}) custom-call(f32[2,512,1024]{2,1,0:T(8,128)} %get-tuple-element.9.ga, f32[2,512,1024]{2,1,0:T(8,128)} %get-tuple-element.10.gbt, f32[8,128]{1,0:T(8,128)} %get-tuple-element.11.loss), custom_call_target="tpu_custom_call" | custom-call | tf_op jit(solution)/shard_map/pallas_call | solution.py:380

commit v7 on v6

--- a/solution.py
+++ b/solution.py
@@ -16,7 +16,7 @@
 SENDS = 4
 PAIR_SLACK = 2
 CHIP_SLACK = 5
-NEAR = 8
+NEAR = 7
 HALVES = 2
 LATE = 4
 SPLIT = 2
@@ -289,6 +289,32 @@
             run(fwd_steps(t, whole, tokens))
             each(t, ship_fwd)
 
+        @pl.when((i == num_micro) & (near == False))
+        def _():
+            store_e(num_micro - 1).wait()
+            load_e(0).start()
+
+        @pl.when(does_w & (which == 0) & near)
+        def _():
+            wgt(k, 0, True)
+
+        @pl.when(does_w & (which == 0) & (near == False))
+        def _():
+            @pl.when(k + 2 < num_micro)
+            def _():
+                load_e(k + 2).start()
+            load_e(k).wait()
+            wgt(k, 0, False)
+
+        @pl.when(does_w & (which == 1))
+        def _():
+            wgt(k, 1, True)
+
+        for pick in range(2):
+            @pl.when((k >= num_micro - 4) & (which == pick))
+            def _(pick=pick):
+                result(k, pick).start()
+
         @pl.when(i == num_micro - 1)
         def _():
             @pl.when(is_last == False)
@@ -320,32 +346,6 @@
             @pl.when(i > 0)
             def _():
                 store_e(i - 1).wait()
-
-        @pl.when((i == num_micro) & (near == False))
-        def _():
-            store_e(num_micro - 1).wait()
-            load_e(0).start()
-
-        @pl.when(does_w & (which == 0) & near)
-        def _():
-            wgt(k, 0, True)
-
-        @pl.when(does_w & (which == 0) & (near == False))
-        def _():
-            @pl.when(k + 2 < num_micro)
-            def _():
-                load_e(k + 2).start()
-            load_e(k).wait()
-            wgt(k, 0, False)
-
-        @pl.when(does_w & (which == 1))
-        def _():
-            wgt(k, 1, True)
-
-        for pick in range(2):
-            @pl.when((k >= num_micro - 4) & (which == pick))
-            def _(pick=pick):
-                result(k, pick).start()
 
         return carry
 

time: 296 us -> 297 us (level)
  no operation moved by 1% of the time
where the time goes in v7:
time: 297 us; the launch traced here: 295 us
  Pallas kernels  294 us (99%)
    pallas_call x1, Pallas kernels, per_device(): pl.pallas_call(functools.partial(kernel, stages, num_micro, ring), out_sh...  287 us
    pallas_call x1, Pallas kernels, write_results(): pl.pallas_call(finish, grid=(layers, SPLIT), in_specs=[pl.BlockSpec((1, r...  7.42 us

profile of v7, /device:TPU:96, one launch (start us, length us, event | category | flops | bytes accessed | tf_op | source)
XLA Modules:
  0.0 294.6 jit_solution(7158379853668299978)
XLA Ops:
  0.6 286.5 %shard_map.67 = (f32[2,512,1024]{2,1,0:T(8,128)}, f32[2,512,1024]{2,1,0:T(8,128)}, f32[8,128]{1,0:T(8,128)}, bf16[2,32,128,1024]{3,2,1,0:T(8,128)(2,1)}) custom-call(bf16[32,128,512]{2,1,0:T(8,128)(2,1)} %x_hbm.1, bf16[32,128,512]{2,1,0:T(8,128)(2,1)} %t_hbm.1, bf16[2,512,1024]{2,1,0:T(8,128)(2,1)} %bitcast.4, bf16[2,1024,512]{2,1,0:T(8,128)(2,1)} %bitcast.5), custom_call_target="tpu_custom_call" | custom-call | tf_op jit(solution)/shard_map/pallas_call | solution.py:398
  287.2 7.4 %shard_map.68 = (f32[2,512,1024]{2,1,0:T(8,128)}, f32[2,1024,512]{2,1,0:T(8,128)}, f32[1]{0:T(128)}) custom-call(f32[2,512,1024]{2,1,0:T(8,128)} %get-tuple-element.9.ga, f32[2,512,1024]{2,1,0:T(8,128)} %get-tuple-element.10.gbt, f32[8,128]{1,0:T(8,128)} %get-tuple-element.11.loss), custom_call_target="tpu_custom_call" | custom-call | tf_op jit(solution)/shard_map/pallas_call | solution.py:380
